TPU v7x, 128 devices: a whole 4x4x4 slice. The times are simulated.
128 devices in a mesh: row: 8 (over z, core), col: 16 (over y, x).
Axes of the slice: x: 4, y: 4, z: 4, core: 2. Of those that a mesh axis runs over, the one named last changes fastest.
Arguments:
- features: bfloat16 [131072, 256], P(('row', 'col')), may hold values from -6 to 6
- tile_values: bfloat16 [8, 16, 256, 128, 128], P('row', 'col'), may hold values from -0.09375 to 0.09375
- tile_rows: int32 [8, 16, 256], P('row', 'col'), may hold values from 0 to 127, as said below
- tile_cols: int32 [8, 16, 256], P('row', 'col'), may hold values from 0 to 63, as said below
- tile_count: int32 [8, 16], P('row', 'col'), may hold values from 64 to 256, as said below
- w_first: bfloat16 [256, 256], replicated, may hold values from -0.375 to 0.375
- w_second: bfloat16 [256, 256], replicated, may hold values from -0.375 to 0.375
Outputs:
- output: bfloat16 [131072, 256], P(('row', 'col'))
Inputs may be any that keep to these rules, and one draw needn't show every extreme that they name: `tile_rows`: in each block the slots name distinct tiles; the first tile_count slots are ordered by tile column, then tile row; later slots are padding. `tile_cols`: as for tile_rows. `tile_count`: some block uses all 256 slots.
All inputs are finite; a program needn't handle non-finite values.
Results may differ from a plain program's by a relative error of at most 0.024.
Values may be sent and summed in bfloat16 or wider, within the bound.
A program may use at most 192 MiB of HBM per device.

v0:
```python
import jax
import jax.numpy as jnp
from jax import lax
from jax.sharding import PartitionSpec as P

GROUP = 64


def order_by(primary, secondary, stride, occupied, beyond):
    slot_ids = jnp.arange(primary.shape[0], dtype=jnp.int32)
    marked = jnp.where(occupied, primary * stride + secondary, beyond + slot_ids)
    slot_order = jnp.argsort(marked, stable=True)
    return (slot_order, marked[slot_order])


def accumulate(
    running, layout, slot_order, order_keys, key_low, key_high, panel_tiles, col_base, row_base
):
    values, row_ids, col_ids = layout
    group_size = GROUP
    first_pos = jnp.sum(order_keys < key_low)
    last_pos = jnp.sum(order_keys < key_high)
    group_low = first_pos // group_size
    group_high = (last_pos + group_size - 1) // group_size
    out_tiles = running.shape[0]
    tile_size = running.shape[1]
    feature_width = running.shape[2]
    out_ids = jnp.arange(out_tiles, dtype=jnp.int32)

    def group_step(group_index, current):
        positions = group_index * group_size + jnp.arange(group_size, dtype=jnp.int32)
        slot_ids = slot_order[positions]
        active = (positions >= first_pos) & (positions < last_pos)
        source = jnp.clip(col_ids[slot_ids] - col_base, 0, panel_tiles.shape[0] - 1)
        target = row_ids[slot_ids] - row_base
        products = jnp.einsum(
            "gij,gjf->gif",
            values[slot_ids],
            panel_tiles[source],
            preferred_element_type=jnp.float32,
        )
        flat = products.reshape(group_size, tile_size * feature_width)
        high = flat.astype(jnp.bfloat16)
        low = (flat - high.astype(jnp.float32)).astype(jnp.bfloat16)
        selector = ((out_ids[:, None] == target[None, :]) & active[None, :]).astype(jnp.bfloat16)
        placed = jnp.dot(selector, high, preferred_element_type=jnp.float32)
        placed = placed + jnp.dot(selector, low, preferred_element_type=jnp.float32)
        return current + placed.reshape(out_tiles, tile_size, feature_width)

    return lax.fori_loop(group_low, group_high, group_step, running)


def propagate(inputs_now, weight, layout, by_column, row_tiles, col_tiles):
    node_dev, feature_width = inputs_now.shape
    tile_size = layout[0].shape[-1]
    zeroes = jnp.zeros((row_tiles, tile_size, feature_width), jnp.float32)
    panel_tiles = lax.all_gather(inputs_now, "row", axis=0, tiled=True).reshape(
        -1, tile_size, feature_width
    )
    partial_value = accumulate(
        zeroes, layout, by_column[0], by_column[1], 0, row_tiles * col_tiles, panel_tiles, 0, 0
    )
    rounded = partial_value.reshape(-1, feature_width).astype(jnp.bfloat16)
    summed = lax.psum_scatter(rounded, "col", scatter_dimension=0, tiled=True).astype(jnp.float32)
    aggregated = summed.astype(jnp.bfloat16)
    return jax.nn.relu(jnp.dot(aggregated, weight, preferred_element_type=jnp.float32)).astype(
        jnp.bfloat16
    )


def shards(features, tile_values, tile_rows, tile_cols, tile_count, w_first, w_second):
    tile_size = tile_values.shape[-1]
    values = tile_values[0, 0]
    row_ids = tile_rows[0, 0]
    col_ids = tile_cols[0, 0]
    filled = tile_count[0, 0]
    node_dev = features.shape[0]
    row_tiles = node_dev * lax.axis_size("col") // tile_size
    col_tiles = node_dev * lax.axis_size("row") // tile_size
    occupied = jnp.arange(values.shape[0], dtype=jnp.int32) < filled
    beyond = row_tiles * col_tiles
    by_column = order_by(col_ids, row_ids, row_tiles, occupied, beyond)
    layout = (values, row_ids, col_ids)
    hidden = propagate(features, w_first, layout, by_column, row_tiles, col_tiles)
    return propagate(hidden, w_second, layout, by_column, row_tiles, col_tiles)


def solution(mesh):
    return jax.shard_map(
        shards,
        mesh=mesh,
        in_specs=(
            P(("row", "col"), None),
            P("row", "col", None, None, None),
            P("row", "col", None),
            P("row", "col", None),
            P("row", "col"),
            P(),
            P(),
        ),
        out_specs=P(("row", "col"), None),
        check_vma=False,
    )
```

profile of v0, /device:TPU:0, one launch (start us, length us, event | category | flops | bytes accessed | tf_op | source)
XLA Modules:
  0.0 791.9 jit_solution(5772972226902755362)
XLA Ops:
  17.6 26.3 %all-gather.3.cloned.1.call-done = bf16[8192,256]{1,0:T(8,128)(2,1)} async-done(((bf16[1024,256]{1,0:T(8,128)(2,1)}), bf16[8192,256]{1,0:T(8,128)(2,1)}) %all-gather.3.cloned.1.call-update) | async-done | bytes 4194320 | tf_op jit(solution)/shard_map/all_gather | solution.py:57
  43.9 7.8 broadcast.197.clone
  51.7 187.6 %while.22 = (s32[]{:T(128)}, f32[128,128,256]{2,1,0:T(8,128)}, s32[]{:T(128)}, s32[256]{0:T(256)S(1)}, s32[256]{0:T(256)S(1)}, /*index=5*/s32[]{:T(128)}, s32[]{...) while((s32[]{:T(128)}, f32[128,128,256]{2,1,0:T(8,128)}, ...), condition=%wide.region_4.5_spmd.clone, body=%wide.region_3.4_spmd.clone.sunk | while | flops 1629523968 | bytes 195053136 | solution.py:50
  55.3 4.3 gather_fusion.1
  59.7 4.9 gather_fusion.3
  68.1 4.7 copy.16
  72.8 8.0 %fusion.73 = f32[128,32768]{1,0:T(8,128)} fusion(f32[64,32768]{1,0:T(8,128)S(1)} %bitcast.95, s32[64]{0:T(128)S(1)} %gather_fusion.4, pred[64]{0:T(512)(128)(4,1)S(1)} %compare_and_fusion.4), kind=kOutput, calls=%fused_computation.17.clone.1 | convolution fusion | flops 538984448 | bytes 25166144 | tf_op jit(solution)/shard_map/while/body/dot_general | solution.py:46
  80.8 10.5 %convolution_add_fusion.4 = f32[128,32768]{1,0:T(8,128)} fusion(f32[128,32768]{1,0:T(8,128)} %fusion.73, f32[64,32768]{1,0:T(8,128)S(1)} %bitcast.96, s32[64]{0:T(128)S(1)} %gather_fusion.4, pred[64]{0:T(512)(128)(4,1)S(1)} %compare_and_fusion.4), kind=kOutput, calls=%fused_computation.13.clone.1 | convolution fusion | flops 549470208 | bytes 41943360 | tf_op jit(solution)/shard_map/while/body/dot_general | solution.py:47
  91.3 10.9 %copy.17 = f32[16,8,128,256]{3,2,1,0:T(8,128)S(1)} copy(f32[16,8,128,256]{3,1,2,0:T(8,128)} %bitcast.99) | data formatting | bytes 33554432 | tf_op jit(solution)/shard_map/while
  102.2 12.1 %bitcast_add_fusion.4 = f32[128,128,256]{2,1,0:T(8,128)} fusion(f32[128,128,256]{2,1,0:T(8,128)} %get-tuple-element.350, f32[16,8,128,256]{3,2,1,0:T(8,128)S(1)} %copy.17), kind=kLoop, calls=%fused_computation.14.clone.1 | loop fusion | flops 4194304 | bytes 50331648 | tf_op jit(solution)/shard_map/while/body/add | solution.py:48
  117.9 4.3 gather_fusion.1
  122.2 4.9 gather_fusion.3
  130.6 4.7 copy.16
  135.3 8.0 %fusion.73 = f32[128,32768]{1,0:T(8,128)} fusion(f32[64,32768]{1,0:T(8,128)S(1)} %bitcast.95, s32[64]{0:T(128)S(1)} %gather_fusion.4, pred[64]{0:T(512)(128)(4,1)S(1)} %compare_and_fusion.4), kind=kOutput, calls=%fused_computation.17.clone.1 | convolution fusion | flops 538984448 | bytes 25166144 | tf_op jit(solution)/shard_map/while/body/dot_general | solution.py:46
  143.4 10.5 %convolution_add_fusion.4 = f32[128,32768]{1,0:T(8,128)} fusion(f32[128,32768]{1,0:T(8,128)} %fusion.73, f32[64,32768]{1,0:T(8,128)S(1)} %bitcast.96, s32[64]{0:T(128)S(1)} %gather_fusion.4, pred[64]{0:T(512)(128)(4,1)S(1)} %compare_and_fusion.4), kind=kOutput, calls=%fused_computation.13.clone.1 | convolution fusion | flops 549470208 | bytes 41943360 | tf_op jit(solution)/shard_map/while/body/dot_general | solution.py:47
  153.8 10.9 %copy.17 = f32[16,8,128,256]{3,2,1,0:T(8,128)S(1)} copy(f32[16,8,128,256]{3,1,2,0:T(8,128)} %bitcast.99) | data formatting | bytes 33554432 | tf_op jit(solution)/shard_map/while
  164.7 12.1 %bitcast_add_fusion.4 = f32[128,128,256]{2,1,0:T(8,128)} fusion(f32[128,128,256]{2,1,0:T(8,128)} %get-tuple-element.350, f32[16,8,128,256]{3,2,1,0:T(8,128)S(1)} %copy.17), kind=kLoop, calls=%fused_computation.14.clone.1 | loop fusion | flops 4194304 | bytes 50331648 | tf_op jit(solution)/shard_map/while/body/add | solution.py:48
  184.8 4.9 gather_fusion.3
  193.1 4.7 copy.16
  197.9 8.0 %fusion.73 = f32[128,32768]{1,0:T(8,128)} fusion(f32[64,32768]{1,0:T(8,128)S(1)} %bitcast.95, s32[64]{0:T(128)S(1)} %gather_fusion.4, pred[64]{0:T(512)(128)(4,1)S(1)} %compare_and_fusion.4), kind=kOutput, calls=%fused_computation.17.clone.1 | convolution fusion | flops 538984448 | bytes 25166144 | tf_op jit(solution)/shard_map/while/body/dot_general | solution.py:46
  205.9 10.5 %convolution_add_fusion.4 = f32[128,32768]{1,0:T(8,128)} fusion(f32[128,32768]{1,0:T(8,128)} %fusion.73, f32[64,32768]{1,0:T(8,128)S(1)} %bitcast.96, s32[64]{0:T(128)S(1)} %gather_fusion.4, pred[64]{0:T(512)(128)(4,1)S(1)} %compare_and_fusion.4), kind=kOutput, calls=%fused_computation.13.clone.1 | convolution fusion | flops 549470208 | bytes 41943360 | tf_op jit(solution)/shard_map/while/body/dot_general | solution.py:47
  216.3 10.9 %copy.17 = f32[16,8,128,256]{3,2,1,0:T(8,128)S(1)} copy(f32[16,8,128,256]{3,1,2,0:T(8,128)} %bitcast.99) | data formatting | bytes 33554432 | tf_op jit(solution)/shard_map/while
  227.2 12.1 %bitcast_add_fusion.4 = f32[128,128,256]{2,1,0:T(8,128)} fusion(f32[128,128,256]{2,1,0:T(8,128)} %get-tuple-element.350, f32[16,8,128,256]{3,2,1,0:T(8,128)S(1)} %copy.17), kind=kLoop, calls=%fused_computation.14.clone.1 | loop fusion | flops 4194304 | bytes 50331648 | tf_op jit(solution)/shard_map/while/body/add | solution.py:48
  239.3 9.0 %convert_element_type.52 = bf16[128,128,256]{2,1,0:T(8,128)(2,1)} convert(f32[128,128,256]{2,1,0:T(8,128)} %get-tuple-element.123) | non-fusion elementwise | flops 4194304 | bytes 25165824 | tf_op jit(solution)/shard_map/convert_element_type | solution.py:63
  248.4 148.1 %reduce-scatter.3.cloned.1.call-done = bf16[1024,256]{1,0:T(8,128)(2,1)} async-done(((bf16[16384,256]{1,0:T(8,128)(2,1)}), bf16[1024,256]{1,0:T(8,128)(2,1)}) %reduce-scatter.3.cloned.1.call-update) | async-done | bytes 524304 | tf_op jit(solution)/shard_map/reduce_scatter | solution.py:64
  398.7 31.8 %all-gather.5.cloned.1.call-done = bf16[8192,256]{1,0:T(8,128)(2,1)} async-done(((bf16[1024,256]{1,0:T(8,128)(2,1)}), bf16[8192,256]{1,0:T(8,128)(2,1)}) %all-gather.5.cloned.1.call-update) | async-done | bytes 4194320 | tf_op jit(solution)/shard_map/all_gather | solution.py:57
  430.6 7.8 broadcast.197
  438.4 187.6 %while.23 = (s32[]{:T(128)}, f32[128,128,256]{2,1,0:T(8,128)}, s32[]{:T(128)}, s32[256]{0:T(256)S(1)}, s32[256]{0:T(256)S(1)}, /*index=5*/s32[]{:T(128)}, s32[]{...) while((s32[]{:T(128)}, f32[128,128,256]{2,1,0:T(8,128)}, ...), condition=%wide.region_7.8_spmd.clone, body=%wide.region_6.7_spmd.clone.sunk | while | flops 1629523968 | bytes 195053136 | solution.py:50
  446.4 4.9 gather_fusion.8
  454.8 4.7 copy.18
  459.5 8.0 %fusion.83 = f32[128,32768]{1,0:T(8,128)} fusion(f32[64,32768]{1,0:T(8,128)S(1)} %bitcast.97, s32[64]{0:T(128)S(1)} %gather_fusion.9, pred[64]{0:T(512)(128)(4,1)S(1)} %compare_and_fusion.5), kind=kOutput, calls=%fused_computation.39.clone.1 | convolution fusion | flops 538984448 | bytes 25166144 | tf_op jit(solution)/shard_map/while/body/dot_general | solution.py:46
  467.5 10.5 %convolution_add_fusion.5 = f32[128,32768]{1,0:T(8,128)} fusion(f32[128,32768]{1,0:T(8,128)} %fusion.83, f32[64,32768]{1,0:T(8,128)S(1)} %bitcast.98, s32[64]{0:T(128)S(1)} %gather_fusion.9, pred[64]{0:T(512)(128)(4,1)S(1)} %compare_and_fusion.5), kind=kOutput, calls=%fused_computation.35.clone.1 | convolution fusion | flops 549470208 | bytes 41943360 | tf_op jit(solution)/shard_map/while/body/dot_general | solution.py:47
  478.0 10.9 %copy.19 = f32[16,8,128,256]{3,2,1,0:T(8,128)S(1)} copy(f32[16,8,128,256]{3,1,2,0:T(8,128)} %bitcast.100) | data formatting | bytes 33554432 | tf_op jit(solution)/shard_map/while
  488.9 12.1 %bitcast_add_fusion.5 = f32[128,128,256]{2,1,0:T(8,128)} fusion(f32[128,128,256]{2,1,0:T(8,128)} %get-tuple-element.386, f32[16,8,128,256]{3,2,1,0:T(8,128)S(1)} %copy.19), kind=kLoop, calls=%fused_computation.36.clone.1 | loop fusion | flops 4194304 | bytes 50331648 | tf_op jit(solution)/shard_map/while/body/add | solution.py:48
  508.9 4.9 gather_fusion.8
  517.3 4.7 copy.18
  522.0 8.0 %fusion.83 = f32[128,32768]{1,0:T(8,128)} fusion(f32[64,32768]{1,0:T(8,128)S(1)} %bitcast.97, s32[64]{0:T(128)S(1)} %gather_fusion.9, pred[64]{0:T(512)(128)(4,1)S(1)} %compare_and_fusion.5), kind=kOutput, calls=%fused_computation.39.clone.1 | convolution fusion | flops 538984448 | bytes 25166144 | tf_op jit(solution)/shard_map/while/body/dot_general | solution.py:46
  530.1 10.4 %convolution_add_fusion.5 = f32[128,32768]{1,0:T(8,128)} fusion(f32[128,32768]{1,0:T(8,128)} %fusion.83, f32[64,32768]{1,0:T(8,128)S(1)} %bitcast.98, s32[64]{0:T(128)S(1)} %gather_fusion.9, pred[64]{0:T(512)(128)(4,1)S(1)} %compare_and_fusion.5), kind=kOutput, calls=%fused_computation.35.clone.1 | convolution fusion | flops 549470208 | bytes 41943360 | tf_op jit(solution)/shard_map/while/body/dot_general | solution.py:47
  540.5 10.9 %copy.19 = f32[16,8,128,256]{3,2,1,0:T(8,128)S(1)} copy(f32[16,8,128,256]{3,1,2,0:T(8,128)} %bitcast.100) | data formatting | bytes 33554432 | tf_op jit(solution)/shard_map/while
  551.4 12.1 %bitcast_add_fusion.5 = f32[128,128,256]{2,1,0:T(8,128)} fusion(f32[128,128,256]{2,1,0:T(8,128)} %get-tuple-element.386, f32[16,8,128,256]{3,2,1,0:T(8,128)S(1)} %copy.19), kind=kLoop, calls=%fused_computation.36.clone.1 | loop fusion | flops 4194304 | bytes 50331648 | tf_op jit(solution)/shard_map/while/body/add | solution.py:48
  571.5 4.9 gather_fusion.8
  579.8 4.7 copy.18
  584.6 8.0 %fusion.83 = f32[128,32768]{1,0:T(8,128)} fusion(f32[64,32768]{1,0:T(8,128)S(1)} %bitcast.97, s32[64]{0:T(128)S(1)} %gather_fusion.9, pred[64]{0:T(512)(128)(4,1)S(1)} %compare_and_fusion.5), kind=kOutput, calls=%fused_computation.39.clone.1 | convolution fusion | flops 538984448 | bytes 25166144 | tf_op jit(solution)/shard_map/while/body/dot_general | solution.py:46
  592.6 10.5 %convolution_add_fusion.5 = f32[128,32768]{1,0:T(8,128)} fusion(f32[128,32768]{1,0:T(8,128)} %fusion.83, f32[64,32768]{1,0:T(8,128)S(1)} %bitcast.98, s32[64]{0:T(128)S(1)} %gather_fusion.9, pred[64]{0:T(512)(128)(4,1)S(1)} %compare_and_fusion.5), kind=kOutput, calls=%fused_computation.35.clone.1 | convolution fusion | flops 549470208 | bytes 41943360 | tf_op jit(solution)/shard_map/while/body/dot_general | solution.py:47
  603.0 10.9 %copy.19 = f32[16,8,128,256]{3,2,1,0:T(8,128)S(1)} copy(f32[16,8,128,256]{3,1,2,0:T(8,128)} %bitcast.100) | data formatting | bytes 33554432 | tf_op jit(solution)/shard_map/while
  613.9 12.1 %bitcast_add_fusion.5 = f32[128,128,256]{2,1,0:T(8,128)} fusion(f32[128,128,256]{2,1,0:T(8,128)} %get-tuple-element.386, f32[16,8,128,256]{3,2,1,0:T(8,128)S(1)} %copy.19), kind=kLoop, calls=%fused_computation.36.clone.1 | loop fusion | flops 4194304 | bytes 50331648 | tf_op jit(solution)/shard_map/while/body/add | solution.py:48
  626.0 9.0 %convert_element_type.55 = bf16[128,128,256]{2,1,0:T(8,128)(2,1)} convert(f32[128,128,256]{2,1,0:T(8,128)} %get-tuple-element.124) | non-fusion elementwise | flops 4194304 | bytes 25165824 | tf_op jit(solution)/shard_map/convert_element_type | solution.py:63
  635.1 148.2 %reduce-scatter.5.cloned.1.call-done = bf16[1024,256]{1,0:T(8,128)(2,1)} async-done(((bf16[16384,256]{1,0:T(8,128)(2,1)}), bf16[1024,256]{1,0:T(8,128)(2,1)}) %reduce-scatter.5.cloned.1.call-update) | async-done | bytes 524304 | tf_op jit(solution)/shard_map/reduce_scatter | solution.py:64
  (97 shorter events, 71.3 us)
Async XLA Ops:
  6.5 390.0 %copy-start = (bf16[256,256]{1,0:T(8,128)(2,1)S(1)}, bf16[256,256]{1,0:T(8,128)(2,1)}, u32[]{:S(2)}) copy-start(bf16[256,256]{1,0:T(8,128)(2,1)} %param.16) | copy-start | bytes 393220
  6.5 37.3 %all-gather.3.cloned.1.call-start = ((), (), s32[]{:S(2)}) async-start(), calls=%async_computation.2 | async-start | bytes 4718592 | tf_op jit(solution)/shard_map/all_gather | solution.py:57
  7.3 389.3 %reduce-scatter.3.cloned.1.call-start = ((), (), s32[]{:S(2)}) async-start(), calls=%async_computation.3 | async-start | bytes 8912896 | tf_op jit(solution)/shard_map/reduce_scatter | solution.py:64
  43.9 7.8 copy-start.2
  43.9 7.8 copy-start.3
  248.3 182.2 %all-gather.5.cloned.1.call-start = ((), (), s32[]{:S(2)}) async-start(), calls=%async_computation.4 | async-start | bytes 4718592 | tf_op jit(solution)/shard_map/all_gather | solution.py:57
  398.7 384.6 %reduce-scatter.5.cloned.1.call-start = ((), (), s32[]{:S(2)}) async-start(), calls=%async_computation.5 | async-start | bytes 8912896 | tf_op jit(solution)/shard_map/reduce_scatter | solution.py:64
  626.0 159.4 %copy-start.1 = (bf16[256,256]{1,0:T(8,128)(2,1)S(1)}, bf16[256,256]{1,0:T(8,128)(2,1)}, u32[]{:S(2)}) copy-start(bf16[256,256]{1,0:T(8,128)(2,1)} %param.16) | copy-start | bytes 393220
  635.1 148.2 %copy-start.4 = (bf16[256,256]{1,0:T(8,128)(2,1)S(1)}, bf16[256,256]{1,0:T(8,128)(2,1)}, u32[]{:S(2)}) copy-start(bf16[256,256]{1,0:T(8,128)(2,1)} %param.17) | copy-start | bytes 393220
Sparse Core Ops, SparseCore 0:
  9.0 34.7 all-gather.2
  248.5 148.0 reduce-scatter.2
  398.8 31.7 all-gather.4
  635.2 148.0 reduce-scatter.4
where the time goes:
time: 794 us; the launch traced here: 792 us
  waiting for transfers between devices  355 us (45%)
  local copies, waits for them, and re-layouts  181 us (23%)
  matrix products  136 us (17%)
  other arithmetic  102 us (13%)
  between operations  16.9 us (2%)
    reduce_scatter x2, waiting for transfers between devices, propagate(): lax.psum_scatter(rounded, 'col', scatter_dimension=0, tiled=True)  296 us
    while x12, local copies, waits for them, and re-layouts  93.7 us
    add x6, other arithmetic, group_step(): return current + placed.reshape(out_tiles, tile_size, feature_width)  72.4 us
    dot_general x6, matrix products, group_step(): placed = placed + jnp.dot(selector, low, preferred_element_type=jnp.float32)  62.7 us
    all_gather x2, waiting for transfers between devices, propagate(): lax.all_gather(inputs_now, 'row', axis=0, tiled=True)  58.1 us
    dot_general x6, matrix products, group_step(): placed = jnp.dot(selector, high, preferred_element_type=jnp.float32)  48.1 us
    gather x6, local copies, waits for them, and re-layouts, group_step(): panel_tiles[source]  29.6 us
    gather x6, local copies, waits for them, and re-layouts, group_step(): values[slot_ids]  26 us
  transfers between devices with their start and end apart: 4, of which 4 were waited for; matrix products, arithmetic and copies ran while one was open for 1% of the time, Pallas kernels for 0%

commit v1 on v0

v1 whole, which is shorter than its diff:
```python
import functools

import jax
import jax.numpy as jnp
from jax import lax
from jax.experimental import pallas as pl
from jax.experimental.pallas import tpu as pltpu
from jax.sharding import PartitionSpec as P

MESH = pl.DeviceIdType.MESH
F = 256
TILE = 128
SLOTS = 256
ROW_TILES = 128
COL_TILES = 64
NODES = 1024
PIECE = 256
SIDE = 4
OFFSETS = (2, 1, 3, 0)
FAR, RAW, MERGED = 0, 1, 2


def remote(src, dst, send, recv, row, col):
    return pltpu.make_async_remote_copy(
        src_ref=src, dst_ref=dst, send_sem=send, recv_sem=recv, device_id=(row, col), device_id_type=MESH
    )


def greet(partners):
    barrier = pltpu.get_barrier_semaphore()
    for row, col in partners:
        pl.semaphore_signal(barrier, inc=1, device_id=(row, col), device_id_type=MESH)
    pl.semaphore_wait(barrier, len(partners))


def gather_kernel(x_hbm, panel_hbm, held, send, recv, mate_send, mate_recv, local, out_sem):
    row, col = lax.axis_index("row"), lax.axis_index("col")
    z, core = row // 2, row % 2
    mate = z * 2 + 1 - core
    half = NODES // 2
    steps = ((z + 1) % SIDE * 2 + core, (z + 3) % SIDE * 2 + core)
    load = pltpu.make_async_copy(x_hbm, held.at[row], local)
    load.start()
    greet([(steps[0], col), (steps[1], col), (mate, col)])
    load.wait()

    def part(block, which):
        return held.at[block, pl.ds(which * half, half)]

    def hop(way, order, block, which):
        piece = part(block, which)
        return remote(piece, piece, send.at[way, order], recv.at[way, order], steps[way], col)

    def share(order, block, which):
        piece = part(block, which)
        return remote(piece, piece, mate_send.at[order], mate_recv.at[order], mate, col)

    def put(order, block, which):
        piece = part(block, which)
        return pltpu.make_async_copy(piece, panel_hbm.at[block, pl.ds(which * half, half)], out_sem.at[order])

    def at(distance, k):
        return (z + distance) % SIDE * 2 + k

    own = ((0, 0), (0, 1))
    first = ((3, 0), (1, 1))
    second = ((3, 1), (1, 0))
    last = ((2, 0), (2, 1))
    pieces = own + first + second + last
    started = []

    def begin(copy):
        copy.start()
        started.append(copy)

    for order in range(2):
        for way in range(2):
            begin(hop(way, order, row, way ^ order))
    for order in range(2):
        begin(share(order, row, order))
        begin(put(order, row, order))
    count = 2
    for order, group in enumerate((first, second, last)):
        for way in range(2):
            distance, which = group[way]
            block = at(distance, core)
            hop(way, order, block, which).wait_recv()
            if order == 0:
                begin(hop(way, 2, block, which))
            begin(share(count, block, which))
            begin(put(count, block, which))
            count += 1
    for order in range(8):
        distance, which = pieces[order]
        block = at(distance, 1 - core)
        share(order, block, which).wait_recv()
        begin(put(8 + order, block, which))
    for copy in started:
        if copy.is_remote:
            copy.wait_send()
        else:
            copy.wait()


def gather(x, number):
    return pl.pallas_call(
        gather_kernel,
        out_shape=jax.ShapeDtypeStruct((8, NODES, F), jnp.bfloat16),
        in_specs=[pl.BlockSpec(memory_space=pl.ANY)],
        out_specs=pl.BlockSpec(memory_space=pl.ANY),
        scratch_shapes=[
            pltpu.VMEM((8, NODES, F), jnp.bfloat16),
            pltpu.SemaphoreType.DMA((2, 3)),
            pltpu.SemaphoreType.DMA((2, 3)),
            pltpu.SemaphoreType.DMA((8,)),
            pltpu.SemaphoreType.DMA((8,)),
            pltpu.SemaphoreType.DMA,
            pltpu.SemaphoreType.DMA((16,)),
        ],
        compiler_params=pltpu.CompilerParams(collective_id=number, has_side_effects=True),
        name="gather",
    )(x)


UNROLL = 16
LOADS = 8


def tiles_kernel(rows, cols, count, values_hbm, panel_hbm, out_hbm, values, panel, total, staged, value_sem, panel_sem, out_sem):
    per_load = SLOTS // LOADS
    panel_copy = pltpu.make_async_copy(panel_hbm, panel, panel_sem)
    panel_copy.start()

    def load(g):
        window = pl.ds(g * per_load, per_load)
        return pltpu.make_async_copy(values_hbm.at[window], values.at[window], value_sem.at[g])

    for g in range(LOADS):
        load(g).start()

    @pl.loop(0, ROW_TILES + 1)
    def _(t):
        total[t] = jnp.zeros((TILE, F), jnp.float32)

    panel_copy.wait()
    filled = count[0]
    for g in range(LOADS):
        load(g).wait()

        @pl.loop(0, per_load // UNROLL)
        def _(step):
            base = g * per_load + step * UNROLL
            for u in range(UNROLL):
                slot = base + u
                product = jnp.dot(values[slot], panel[cols[slot]], preferred_element_type=jnp.float32)
                target = jnp.where(slot < filled, rows[slot], ROW_TILES)
                total[target] += product

    per_part = ROW_TILES // 16

    def store(part):
        return pltpu.make_async_copy(
            staged.at[part % 4], out_hbm.at[pl.ds(part * per_part, per_part)], out_sem.at[part % 4]
        )

    for part in range(16):
        if part >= 4:
            store(part - 4).wait()

        @pl.loop(0, per_part)
        def _(t):
            staged[part % 4, t] = total[part * per_part + t].astype(jnp.bfloat16)

        store(part).start()
    for part in range(12, 16):
        store(part).wait()


def tiles(rows, cols, count, values, panel):
    scalar = pl.BlockSpec(memory_space=pltpu.SMEM)
    array = pl.BlockSpec(memory_space=pl.ANY)
    return pl.pallas_call(
        tiles_kernel,
        out_shape=jax.ShapeDtypeStruct((ROW_TILES, TILE, F), jnp.bfloat16),
        in_specs=[scalar, scalar, scalar, array, array],
        out_specs=array,
        scratch_shapes=[
            pltpu.VMEM((SLOTS, TILE, TILE), jnp.bfloat16),
            pltpu.VMEM((COL_TILES, TILE, F), jnp.bfloat16),
            pltpu.VMEM((ROW_TILES + 1, TILE, F), jnp.float32),
            pltpu.VMEM((4, ROW_TILES // 16, TILE, F), jnp.bfloat16),
            pltpu.SemaphoreType.DMA((LOADS,)),
            pltpu.SemaphoreType.DMA,
            pltpu.SemaphoreType.DMA((4,)),
        ],
        compiler_params=pltpu.CompilerParams(vmem_limit_bytes=60 * 2**20),
        name="tiles",
    )(rows, cols, count, values, panel)


def add_up(target, terms):
    @pl.loop(0, PIECE // 64)
    def _(t):
        lines = pl.ds(t * 64, 64)
        total = terms[0][lines].astype(jnp.float32)
        for term in terms[1:]:
            total = total + term[lines].astype(jnp.float32)
        target[lines] = total.astype(target.dtype)


def reduce_kernel(
    part_hbm, w, out, near, own, got1, merged1, result, got2, merged2, summed,
    near_sem, own_sem, send1, recv1, send2, recv2,
):
    row, col = lax.axis_index("row"), lax.axis_index("col")
    y, x = col // SIDE, col % SIDE

    def place(half, first, second):
        return second * SIDE + first if half == 0 else first * SIDE + second

    def spot(half):
        return (x, y) if half == 0 else (y, x)

    def step(at, way):
        return (at + (1 if way == 0 else SIDE - 1)) % SIDE

    def piece(half, first, second, h):
        return part_hbm.at[place(half, first, second), 2 * half + h]

    def loads(half):
        first, second = spot(half)
        made = []
        for q in range(SIDE):
            there = (second + OFFSETS[q]) % SIDE
            for way in range(2):
                made.append(
                    pltpu.make_async_copy(
                        piece(half, step(first, way), there, way), near.at[half, way, q], near_sem.at[half, way, q]
                    )
                )
            for h in range(2):
                made.append(
                    pltpu.make_async_copy(piece(half, first, there, h), own.at[half, q, h], own_sem.at[half, q, h])
                )
        return made

    def hop1(half, way, kind, q):
        first, second = spot(half)
        there = (second + OFFSETS[q]) % SIDE
        if kind == FAR:
            src = piece(half, (first + 2) % SIDE, there, way)
        elif kind == RAW:
            src = piece(half, step(first, way), there, 1 - way)
        else:
            src = merged1.at[half, way, q]
        return remote(
            src, got1.at[half, way, kind, q], send1.at[half, way, kind, q], recv1.at[half, way, kind, q],
            row, place(half, step(first, way), second),
        )

    def hop2(half, way, kind):
        first, second = spot(half)
        if kind == FAR:
            src = result.at[half, 0, way]
        elif kind == RAW:
            src = result.at[half, 1 + way, 1 - way]
        else:
            src = merged2.at[half, way]
        return remote(
            src, got2.at[half, way, kind], send2.at[half, way, kind], recv2.at[half, way, kind],
            row, place(half, first, step(second, way)),
        )

    local = loads(0) + loads(1)
    for copy in local:
        copy.start()
    greet([(row, place(half, step(spot(half)[0], way), spot(half)[1])) for half in range(2) for way in range(2)])
    started = []

    def begin(copy):
        copy.start()
        started.append(copy)

    both = [(half, way) for half in range(2) for way in range(2)]
    for q in range(SIDE):
        for kind in (FAR, RAW):
            for half, way in both:
                begin(hop1(half, way, kind, q))
    for copy in local:
        copy.wait()
    for q in range(SIDE):
        for half, way in both:
            hop1(half, way, FAR, q).wait_recv()
            add_up(merged1.at[half, way, q], [near.at[half, way, q], got1.at[half, way, FAR, q]])
            begin(hop1(half, way, MERGED, q))
    for q in range(3):
        for half in range(2):
            for h in range(2):
                hop1(half, h, MERGED, q).wait_recv()
                hop1(half, 1 - h, RAW, q).wait_recv()
                add_up(
                    result.at[half, q, h],
                    [own.at[half, q, h], got1.at[half, h, MERGED, q], got1.at[half, 1 - h, RAW, q]],
                )
                if q == 0:
                    begin(hop2(half, h, FAR))
                elif h == 2 - q:
                    begin(hop2(half, q - 1, RAW))
    for half, way in both:
        hop2(half, way, FAR).wait_recv()
        add_up(merged2.at[half, way], [result.at[half, 1 + way, way], got2.at[half, way, FAR]])
        begin(hop2(half, way, MERGED))
    for half in range(2):
        for h in range(2):
            hop1(half, h, MERGED, 3).wait_recv()
            hop1(half, 1 - h, RAW, 3).wait_recv()
    for half in range(2):
        for h in range(2):
            hop2(half, h, MERGED).wait_recv()
            hop2(half, 1 - h, RAW).wait_recv()
            add_up(
                summed,
                [
                    own.at[half, 3, h], got1.at[half, h, MERGED, 3], got1.at[half, 1 - h, RAW, 3],
                    got2.at[half, h, MERGED], got2.at[half, 1 - h, RAW],
                ],
            )
            product = jnp.dot(summed[...], w[...], preferred_element_type=jnp.float32)
            out[pl.ds((2 * half + h) * PIECE, PIECE)] = jnp.maximum(product, 0.0).astype(jnp.bfloat16)
    for copy in started:
        copy.wait_send()


def reduce(part, w, number):
    block = (PIECE, F)
    dtype = jnp.bfloat16
    vmem = pl.BlockSpec(memory_space=pltpu.VMEM)
    return pl.pallas_call(
        reduce_kernel,
        out_shape=jax.ShapeDtypeStruct((NODES, F), dtype),
        in_specs=[pl.BlockSpec(memory_space=pl.ANY), vmem],
        out_specs=vmem,
        scratch_shapes=[
            pltpu.VMEM((2, 2, 4) + block, dtype),
            pltpu.VMEM((2, 4, 2) + block, dtype),
            pltpu.VMEM((2, 2, 3, 4) + block, dtype),
            pltpu.VMEM((2, 2, 4) + block, dtype),
            pltpu.VMEM((2, 3, 2) + block, dtype),
            pltpu.VMEM((2, 2, 3) + block, dtype),
            pltpu.VMEM((2, 2) + block, dtype),
            pltpu.VMEM(block, dtype),
            pltpu.SemaphoreType.DMA((2, 2, 4)),
            pltpu.SemaphoreType.DMA((2, 4, 2)),
            pltpu.SemaphoreType.DMA((2, 2, 3, 4)),
            pltpu.SemaphoreType.DMA((2, 2, 3, 4)),
            pltpu.SemaphoreType.DMA((2, 2, 3)),
            pltpu.SemaphoreType.DMA((2, 2, 3)),
        ],
        compiler_params=pltpu.CompilerParams(
            collective_id=number, has_side_effects=True, vmem_limit_bytes=60 * 2**20
        ),
        name="reduce",
    )(part, w)


def shards(features, tile_values, tile_rows, tile_cols, tile_count, w_first, w_second):
    rows, cols, count = tile_rows[0, 0], tile_cols[0, 0], tile_count[0]
    values = tile_values[0, 0]
    current = features
    for layer, weight in enumerate((w_first, w_second)):
        panel = gather(current, 2 * layer)
        part = tiles(rows, cols, count, values, panel.reshape(COL_TILES, TILE, F))
        current = reduce(part.reshape(16, 4, PIECE, F), weight, 2 * layer + 1)
    return current


def solution(mesh):
    return jax.shard_map(
        shards,
        mesh=mesh,
        in_specs=(
            P(("row", "col"), None),
            P("row", "col", None, None, None),
            P("row", "col", None),
            P("row", "col", None),
            P("row", "col"),
            P(),
            P(),
        ),
        out_specs=P(("row", "col"), None),
        check_vma=False,
    )
```

time: 794 us -> 190 us (0.24)
  waiting for transfers between devices: 355 us -> 0 us
  Pallas kernels: 0 us -> 186 us
  local copies, waits for them, and re-layouts: 181 us -> 1.87 us
  matrix products: 136 us -> 0 us
  other arithmetic: 102 us -> 0 us
  between operations: 16.9 us -> 0.7 us
    reduce_scatter x2 -> x0, waiting for transfers between devices: 296 us -> none  [propagate(): lax.psum_scatter(rounded, 'col', scatter_dimension=0, tiled=True)]
    pallas_call x0 -> x6, Pallas kernels: none -> 186 us  [the longest x2 106 us: reduce(): pl.pallas_call(reduce_kernel, out_shape=jax.ShapeDtypeStruct((NODES, F),...]
    dot_general x20 -> x0, matrix products: 136 us -> none  [the longest x6 62.7 us: group_step(): placed = placed + jnp.dot(selector, low, preferred_element_type=jnp.float32)]
    while x12 -> x0, local copies, waits for them, and re-layouts: 93.7 us -> none
    add x6 -> x0, other arithmetic: 72.4 us -> none  [group_step(): return current + placed.reshape(out_tiles, tile_size, feature_width)]
    gather x31 -> x0, local copies, waits for them, and re-layouts: 71.9 us -> none  [the longest x6 29.6 us: group_step(): panel_tiles[source]]
    all_gather x2 -> x0, waiting for transfers between devices: 58.1 us -> none  [propagate(): lax.all_gather(inputs_now, 'row', axis=0, tiled=True)]
    convert_element_type x2 -> x0, other arithmetic: 18.1 us -> none  [propagate(): rounded = partial_value.reshape(-1, feature_width).astype(jnp.bfloat16)]
  transfers between devices with their start and end apart: 4 -> 0, of which waited for: 4 -> 0; matrix products, arithmetic and copies ran while one was open for 1% -> 0% of each run, Pallas kernels for 0% -> 0%
where the time goes in v1:
time: 190 us; the launch traced here: 188 us
  Pallas kernels  186 us (98%)
    pallas_call x2, Pallas kernels, reduce(): pl.pallas_call(reduce_kernel, out_shape=jax.ShapeDtypeStruct((NODES, F),...  106 us
    pallas_call x2, Pallas kernels, gather(): pl.pallas_call(gather_kernel, out_shape=jax.ShapeDtypeStruct((8, NODES, F...  47.6 us
    pallas_call x2, Pallas kernels, tiles(): pl.pallas_call(tiles_kernel, out_shape=jax.ShapeDtypeStruct((ROW_TILES, T...  32.6 us

profile of v1, /device:TPU:0, one launch (start us, length us, event | category | flops | bytes accessed | tf_op | source)
XLA Modules:
  0.0 188.4 jit_solution(9258854616009859021)
XLA Ops:
  0.7 24.8 %gather.2 = bf16[8,1024,256]{2,1,0:T(8,128)(2,1)} custom-call(bf16[1024,256]{1,0:T(8,128)(2,1)} %x_hbm.1), custom_call_target="tpu_custom_call" | custom-call | tf_op jit(solution)/shard_map/gather/pallas_call | solution.py:106
  25.4 16.3 %tiles.2 = bf16[128,128,256]{2,1,0:T(8,128)(2,1)} custom-call(s32[256]{0:T(256)} %bitcast.16, s32[256]{0:T(256)} %bitcast.18, s32[1]{0:T(128)} %bitcast.8.count, bf16[256,128,128]{2,1,0:T(8,128)(2,1)} %bitcast.10, bf16[64,128,256]{2,1,0:T(8,128)(2,1)} %bitcast.15), custom_call_target="tpu_custom_call" | custom-call | tf_op jit(solution)/shard_map/tiles/pallas_call | solution.py:182
  41.7 54.1 %reduce.2.x_hbm = bf16[1024,256]{1,0:T(8,128)(2,1)} custom-call(bf16[16,4,256,256]{3,2,1,0:T(8,128)(2,1)} %bitcast.13, bf16[256,256]{1,0:T(8,128)(2,1)} %w.2), custom_call_target="tpu_custom_call" | custom-call | tf_op jit(solution)/shard_map/reduce/pallas_call | solution.py:338
  95.8 22.8 %gather.3 = bf16[8,1024,256]{2,1,0:T(8,128)(2,1)} custom-call(bf16[1024,256]{1,0:T(8,128)(2,1)} %reduce.2.x_hbm), custom_call_target="tpu_custom_call" | custom-call | tf_op jit(solution)/shard_map/gather/pallas_call | solution.py:106
  118.7 16.3 %tiles.3 = bf16[128,128,256]{2,1,0:T(8,128)(2,1)} custom-call(s32[256]{0:T(256)} %bitcast.17, s32[256]{0:T(256)} %bitcast.19, s32[1]{0:T(128)} %bitcast.9.count, bf16[256,128,128]{2,1,0:T(8,128)(2,1)} %bitcast.11, bf16[64,128,256]{2,1,0:T(8,128)(2,1)} %bitcast.14), custom_call_target="tpu_custom_call" | custom-call | tf_op jit(solution)/shard_map/tiles/pallas_call | solution.py:182
  135.0 51.6 %reduce.3 = bf16[1024,256]{1,0:T(8,128)(2,1)} custom-call(bf16[16,4,256,256]{3,2,1,0:T(8,128)(2,1)} %bitcast.12, bf16[256,256]{1,0:T(8,128)(2,1)} %w.3), custom_call_target="tpu_custom_call" | custom-call | tf_op jit(solution)/shard_map/reduce/pallas_call | solution.py:338
  186.5 1.9 copy.10

commit v2 on v0

v2 whole, which is shorter than its diff:
```python
import jax
import jax.numpy as jnp
from jax import lax
from jax.experimental import pallas as pl
from jax.experimental.pallas import tpu as pltpu
from jax.sharding import PartitionSpec as P

MESH = pl.DeviceIdType.MESH
F = 256
WIDE = 128
TILE = 128
SLOTS = 256
NODES = 1024
SIDE = 4
BLOCK_TILES = NODES // TILE
UNROLL = 32
FAR, RAW, MERGED = 0, 1, 2
BF16 = jnp.bfloat16

UNITS = (
    ((0, 1, 0, 512), (0, 1, 512, 512), (1, 1, 0, 256), (1, 1, 256, 256), (1, 1, 512, 256), (1, 1, 768, 256)),
    ((0, 1, 0, 1024), (1, 1, 0, 512), (1, 1, 512, 512)),
)
SPREADS = (
    ((0, 1, 0, 8), (0, 1, 0, 8)),
    ((0, 2, 0, 2), (0, 2, 2, 2), (0, 2, 4, 2), (0, 2, 6, 2)),
)


def remote(src, dst, send, recv, row, col):
    return pltpu.make_async_remote_copy(
        src_ref=src, dst_ref=dst, send_sem=send, recv_sem=recv, device_id=(row, col), device_id_type=MESH
    )


def await_bytes(sized, sem):
    pltpu.make_async_copy(sized, sized, sem).wait()


class Spread:
    def __init__(self, unit, panel, sems, row, col):
        self.f0, self.nf, self.t0, self.tiles = unit
        self.panel, self.row, self.col = panel, row, col
        self.send, self.recv, self.mate_send, self.mate_recv = sems
        self.z, self.core = row // 2, row % 2
        self.mate = self.z * 2 + 1 - self.core
        self.steps = ((self.z + 1) % SIDE * 2 + self.core, (self.z + 3) % SIDE * 2 + self.core)
        self.groups = (((3, 0), (1, 1)), ((3, 1), (1, 0)), ((2, 0), (2, 1)))

    def at(self, distance, core):
        return (self.z + distance) % SIDE * 2 + core

    def part(self, block, which):
        half = self.tiles // 2
        return self.panel.at[pl.ds(self.f0, self.nf), pl.ds(block * BLOCK_TILES + self.t0 + which * half, half)]

    def sized(self, tiles):
        return self.panel.at[pl.ds(self.f0, self.nf), pl.ds(0, tiles)]

    def hop(self, way, order, block, which):
        piece = self.part(block, which)
        remote(piece, piece, self.send, self.recv.at[order], self.steps[way], self.col).start()

    def share(self, block, which):
        piece = self.part(block, which)
        remote(piece, piece, self.mate_send, self.mate_recv, self.mate, self.col).start()

    def own(self):
        for order in range(2):
            for way in range(2):
                self.hop(way, order, self.row, way ^ order)
        for which in range(2):
            self.share(self.row, which)

    def onward(self, order):
        await_bytes(self.sized(self.tiles), self.recv.at[order])
        for way in range(2):
            distance, which = self.groups[order][way]
            block = self.at(distance, self.core)
            if order == 0:
                self.hop(way, 2, block, which)
            self.share(block, which)

    def finish(self):
        await_bytes(self.sized(4 * self.tiles), self.mate_recv)

    def drain(self):
        await_bytes(self.sized(3 * self.tiles), self.send)
        await_bytes(self.sized(4 * self.tiles), self.mate_send)


class Sum:
    def __init__(self, unit, part, got1, got2, sems, row, col):
        self.f0, self.nf, self.r0, self.rows = unit
        self.quarter = self.rows // 4
        self.part, self.got1, self.got2 = part, got1, got2
        self.send1, self.recv1, self.send2, self.recv2 = sems
        self.row = row
        self.y, self.x = col // SIDE, col % SIDE

    def spot(self, half):
        return (self.x, self.y) if half == 0 else (self.y, self.x)

    def step(self, at, way):
        return (at + (1 if way == 0 else SIDE - 1)) % SIDE

    def place(self, half, first, second):
        return second * SIDE + first if half == 0 else first * SIDE + second

    def lines(self, half, h):
        return pl.ds(self.r0 + (2 * half + h) * self.quarter, self.quarter)

    def group(self, half, first, h):
        halves = pl.ds(self.f0, self.nf)
        if half == 0:
            return self.part.at[halves, :, first, self.lines(half, h)]
        return self.part.at[halves, first, :, self.lines(half, h)]

    def single(self, half, second, h):
        halves = pl.ds(self.f0, self.nf)
        first = self.spot(half)[0]
        if half == 0:
            return self.part.at[halves, second, first, self.lines(half, h)]
        return self.part.at[halves, first, second, self.lines(half, h)]

    def hop1(self, half, way, kind):
        first, second = self.spot(half)
        if kind == FAR:
            src = self.group(half, (first + 2) % SIDE, way)
        elif kind == RAW:
            src = self.group(half, self.step(first, way), 1 - way)
        else:
            src = self.group(half, self.step(first, way), way)
        remote(
            src, self.got1.at[half, way, kind], self.send1, self.recv1.at[half, min(kind, 1)],
            self.row, self.place(half, self.step(first, way), second),
        ).start()

    def hop2(self, half, way, kind):
        first, second = self.spot(half)
        if kind == FAR:
            src = self.single(half, (second + 2) % SIDE, way)
        elif kind == RAW:
            src = self.single(half, self.step(second, way), 1 - way)
        else:
            src = self.single(half, self.step(second, way), way)
        remote(
            src, self.got2.at[half, way, kind], self.send2, self.recv2.at[half, min(kind, 1)],
            self.row, self.place(half, first, self.step(second, way)),
        ).start()

    def arrive(self, got, recv, half, kind):
        kinds = pl.ds(0, 1) if kind == FAR else pl.ds(1, 2)
        await_bytes(got.at[half, :, kinds], recv.at[half, kind])

    both = tuple((half, way) for half in range(2) for way in range(2))

    def open(self, fill):
        for half in range(2):
            fill(self, half, (self.spot(half)[0] + 2) % SIDE)
        for half, way in self.both:
            self.hop1(half, way, FAR)
        for way in range(2):
            for half in range(2):
                fill(self, half, self.step(self.spot(half)[0], way))
        for half, way in self.both:
            self.hop1(half, way, RAW)
        for half in range(2):
            fill(self, half, self.spot(half)[0])

    def merge1(self):
        for half, way in self.both:
            if way == 0:
                self.arrive(self.got1, self.recv1, half, FAR)
            mine = self.group(half, self.step(self.spot(half)[0], way), way)
            got = self.got1.at[half, way, FAR]

            @pl.loop(0, self.nf * SIDE)
            def _(i):
                f, j = i // SIDE, i % SIDE
                mine[f, j] = (mine[f, j].astype(jnp.float32) + got[f, j].astype(jnp.float32)).astype(BF16)

            self.hop1(half, way, MERGED)

    def turn(self):
        for half in range(2):
            second = self.spot(half)[1]
            self.arrive(self.got1, self.recv1, half, RAW)
            for h in range(2):
                mine = self.group(half, self.spot(half)[0], h)
                one, two = self.got1.at[half, h, MERGED], self.got1.at[half, 1 - h, RAW]

                @pl.loop(0, self.nf * (SIDE - 1))
                def _(i):
                    f, j = i // (SIDE - 1), (second + 1 + i % (SIDE - 1)) % SIDE
                    total = mine[f, j].astype(jnp.float32) + one[f, j].astype(jnp.float32)
                    mine[f, j] = (total + two[f, j].astype(jnp.float32)).astype(BF16)

            for way in range(2):
                self.hop2(half, way, FAR)
            for way in range(2):
                self.hop2(half, way, RAW)

    def merge2(self):
        for half, way in self.both:
            if way == 0:
                self.arrive(self.got2, self.recv2, half, FAR)
            mine = self.single(half, self.step(self.spot(half)[1], way), way)
            got = self.got2.at[half, way, FAR]
            for f in range(self.nf):
                mine[f] = (mine[f].astype(jnp.float32) + got[f].astype(jnp.float32)).astype(BF16)
            self.hop2(half, way, MERGED)

    def close(self, summed):
        for half in range(2):
            second = self.spot(half)[1]
            self.arrive(self.got2, self.recv2, half, RAW)
            for h in range(2):
                mine = self.single(half, second, h)
                for f in range(self.nf):
                    total = mine[f].astype(jnp.float32)
                    total = total + self.got1[half, h, MERGED, f, second].astype(jnp.float32)
                    total = total + self.got1[half, 1 - h, RAW, f, second].astype(jnp.float32)
                    total = total + self.got2[half, h, MERGED, f].astype(jnp.float32)
                    total = total + self.got2[half, 1 - h, RAW, f].astype(jnp.float32)
                    summed[self.f0 + f, self.lines(half, h)] = total.astype(BF16)

    def drain(self):
        await_bytes(self.got1, self.send1)
        await_bytes(self.got2, self.send2)


def kernel(x, values_hbm, tile_rows, tile_cols, tile_count, w_first, w_second, out, *scratch):
    scratch = list(scratch)

    def take(number):
        taken = scratch[:number]
        del scratch[:number]
        return taken

    values, runs, part, summed, staged, plan, plan_smem, values_sem, x_sem, plan_sem, out_sem = take(11)
    inputs, hidden = take(2), take(1)[0]
    row, col = lax.axis_index("row"), lax.axis_index("col")
    spreads = [
        [Spread(unit, panel, take(4), row, col) for unit, panel in zip(SPREADS[0], inputs)],
        [Spread(unit, hidden, take(4), row, col) for unit in SPREADS[1]],
    ]
    sums = [[Sum(unit, part, *take(2), take(4), row, col) for unit in UNITS[layer]] for layer in range(2)]

    loads = [
        pltpu.make_async_copy(
            x.at[:, :, pl.ds(f * WIDE, WIDE)], inputs[f].at[0, pl.ds(row * BLOCK_TILES, BLOCK_TILES)], x_sem.at[f]
        )
        for f in range(2)
    ]
    for load in loads:
        load.start()
    values_load = pltpu.make_async_copy(values_hbm.at[0, 0], values, values_sem)
    values_load.start()

    first_spread = spreads[0][0]
    first_sum = sums[0][0]
    partners = [(step, col) for step in first_spread.steps] + [(first_spread.mate, col)]
    for half, way in Sum.both:
        first, second = first_sum.spot(half)
        partners.append((row, first_sum.place(half, first_sum.step(first, way), second)))
    barrier = pltpu.get_barrier_semaphore()
    for to_row, to_col in partners:
        pl.semaphore_signal(barrier, inc=1, device_id=(to_row, to_col), device_id_type=MESH)
    pl.semaphore_wait(barrier, len(partners))
    loads[0].wait()
    spreads[0][0].own()

    lane = lax.broadcasted_iota(jnp.int32, (1, SLOTS), 1)
    key = jnp.where(lane < tile_count[0, 0], tile_rows[0] * 64 + tile_cols[0], lane + 8192)
    across = jnp.broadcast_to(key.astype(jnp.float32), (SLOTS, SLOTS))
    down = jnp.transpose(across)
    rank = jnp.sum(jnp.where(across < down, 1.0, 0.0), axis=1, keepdims=True)
    lanes = lax.broadcasted_iota(jnp.int32, (SLOTS, SLOTS), 1)
    slots = lax.broadcasted_iota(jnp.int32, (SLOTS, SLOTS), 0).astype(jnp.float32)
    chosen = rank == lanes.astype(jnp.float32)
    order = jnp.sum(jnp.where(chosen, slots, 0.0), axis=0, keepdims=True)
    ordered = jnp.sum(jnp.where(chosen, down, 0.0), axis=0, keepdims=True)
    ends = jnp.sum(jnp.where(down < ((lanes + 1) * 64).astype(jnp.float32), 1.0, 0.0), axis=0, keepdims=True)
    rest = jnp.zeros((5, SLOTS), jnp.float32)
    plan[...] = jnp.concatenate([order, ordered, ends, rest], axis=0).astype(jnp.int32)
    for f in range(2):
        runs[f, SLOTS] = jnp.zeros((TILE, WIDE), BF16)
    plan_copy = pltpu.make_async_copy(plan, plan_smem, plan_sem)
    plan_copy.start()

    def multiply(panel, f, f0, first, last, total):
        def block(it, total):
            for u in range(UNROLL):
                at = it * UNROLL + u
                slot = jnp.clip(plan_smem[0, at], 0, SLOTS - 1)
                key = jnp.clip(plan_smem[1, at], 0, 64 * SLOTS - 1)
                before = plan_smem[1, jnp.maximum(at - 1, 0)]
                keep = jnp.where(key // 64 == before // 64, 1.0, 0.0)
                right = panel[f, key % 64]
                total = total * keep + jnp.dot(values[slot], right, preferred_element_type=jnp.float32)
                runs[f0, at] = total.astype(BF16)
            return total

        return lax.fori_loop(first // UNROLL, last // UNROLL, block, total)

    empty = jnp.zeros((TILE, WIDE), jnp.float32)

    def fill(unit, half, first):
        tiles = unit.rows // 2 // TILE
        base = unit.r0 // TILE + half * tiles

        @pl.loop(0, SIDE * tiles)
        def _(i):
            second, t = i // tiles, base + i % tiles
            up, across = (second, first) if half == 0 else (first, second)
            line = (up * SIDE + across) * BLOCK_TILES + t
            end = plan_smem[2, line]
            start = jnp.where(line == 0, 0, plan_smem[2, jnp.maximum(line - 1, 0)])
            run = jnp.clip(jnp.where(end == start, SLOTS, end - 1), 0, SLOTS)
            for f in range(unit.nf):
                part[unit.f0 + f, up, across, pl.ds(pl.multiple_of(t * TILE, TILE), TILE)] = runs[unit.f0 + f, run]

    def weigh(unit, w, store):
        @pl.loop(0, unit.rows // TILE)
        def _(i):
            t = unit.r0 // TILE + i
            lines = pl.ds(pl.multiple_of(t * TILE, TILE), TILE)
            both = jnp.concatenate([summed[0, lines], summed[1, lines]], axis=1)
            product = jnp.dot(both, w[...], preferred_element_type=jnp.float32)
            store(t, jnp.maximum(product, 0.0).astype(BF16))

    def keep_hidden(t, block):
        for f in range(2):
            hidden[f, row * BLOCK_TILES + t] = block[:, f * WIDE : (f + 1) * WIDE]

    def keep_output(t, block):
        staged[pl.ds(pl.multiple_of(t * TILE, TILE), TILE)] = block

    def write(unit):
        lines = pl.ds(unit.r0, unit.rows)
        return pltpu.make_async_copy(staged.at[lines], out.at[lines], out_sem.at[unit.r0 // 512])

    a, b = spreads[0]
    a0, a1, b0, b1, b2, b3 = sums[0]
    g0, g1, g2, g3 = spreads[1]
    a.onward(0)
    loads[1].wait()
    b.own()
    a.onward(1)
    a.onward(2)
    plan_copy.wait()
    values_load.wait()
    a.finish()
    total = multiply(inputs[0], 0, 0, 0, 128, empty)
    b.onward(0)
    total = multiply(inputs[0], 0, 0, 128, 256, total)
    a1.open(fill)
    b.onward(1)
    a0.open(fill)
    b.onward(2)
    b.finish()
    total = multiply(inputs[1], 0, 1, 0, 256, empty)
    a0.merge1()
    b0.open(fill)
    b1.open(fill)
    a0.turn()
    b1.merge1()
    b0.merge1()
    a0.merge2()
    a1.merge1()
    b0.turn()
    b1.turn()
    b2.open(fill)
    b0.merge2()
    a0.close(summed)
    b1.merge2()
    b3.open(fill)
    b2.merge1()
    b1.close(summed)
    weigh(b1, w_first, keep_hidden)
    b0.close(summed)
    g1.own()
    weigh(b0, w_first, keep_hidden)
    g0.own()
    b3.merge1()
    a1.turn()
    b2.turn()
    b3.turn()
    a1.merge2()
    b2.merge2()
    g1.onward(0)
    g0.onward(0)
    b3.merge2()
    a1.close(summed)
    b2.close(summed)
    weigh(b2, w_first, keep_hidden)
    g2.own()
    g0.onward(1)
    g1.onward(1)
    b3.close(summed)
    weigh(b3, w_first, keep_hidden)
    g3.own()
    g0.onward(2)
    g1.onward(2)
    g0.finish()
    g1.finish()
    g2.onward(0)
    g2.onward(1)
    g3.onward(0)
    g3.onward(1)
    g2.onward(2)
    g2.finish()
    g3.onward(2)
    for unit in sums[0]:
        unit.drain()
    g3.finish()

    d, e0, e1 = sums[1]
    total = multiply(hidden, 0, 0, 0, 256, empty)
    d.open(fill)
    total = multiply(hidden, 1, 1, 0, 128, empty)
    d.merge1()
    total = multiply(hidden, 1, 1, 128, 256, total)
    e1.open(fill)
    e0.open(fill)
    e1.merge1()
    e0.merge1()
    d.turn()
    e1.turn()
    e0.turn()
    d.merge2()
    e1.merge2()
    e0.merge2()
    d.close(summed)
    e1.close(summed)
    weigh(e1, w_second, keep_output)
    write(e1).start()
    e0.close(summed)
    weigh(e0, w_second, keep_output)
    write(e0).start()
    for unit in spreads[0] + spreads[1] + sums[1]:
        unit.drain()
    write(e0).wait()
    write(e1).wait()


def both_layers(x, values, rows, cols, count, w_first, w_second):
    vmem, smem = pl.BlockSpec(memory_space=pltpu.VMEM), pl.BlockSpec(memory_space=pltpu.SMEM)
    hbm = pl.BlockSpec(memory_space=pl.ANY)
    dma = pltpu.SemaphoreType.DMA
    scratch = [
        pltpu.VMEM((SLOTS, TILE, TILE), BF16),
        pltpu.VMEM((2, SLOTS + 1, TILE, WIDE), BF16),
        pltpu.VMEM((2, SIDE, SIDE, NODES, WIDE), BF16),
        pltpu.VMEM((2, NODES, WIDE), BF16),
        pltpu.VMEM((NODES, F), BF16),
        pltpu.VMEM((8, SLOTS), jnp.int32),
        pltpu.SMEM((8, SLOTS), jnp.int32),
        dma,
        dma((2,)),
        dma,
        dma((2,)),
    ]
    scratch += [pltpu.VMEM((halves, 64, TILE, WIDE), BF16) for halves in (1, 1, 2)]
    for layer in range(2):
        for _ in SPREADS[layer]:
            scratch += [dma, dma((3,)), dma, dma]
    for layer in range(2):
        for _, nf, _, rows_of in UNITS[layer]:
            scratch += [
                pltpu.VMEM((2, 2, 3, nf, SIDE, rows_of // 4, WIDE), BF16),
                pltpu.VMEM((2, 2, 3, nf, rows_of // 4, WIDE), BF16),
                dma, dma((2, 2)), dma, dma((2, 2)),
            ]
    return pl.pallas_call(
        kernel,
        out_shape=jax.ShapeDtypeStruct((NODES, F), BF16),
        in_specs=[hbm, hbm, vmem, vmem, smem, vmem, vmem],
        out_specs=hbm,
        scratch_shapes=scratch,
        compiler_params=pltpu.CompilerParams(
            collective_id=0, has_side_effects=True, vmem_limit_bytes=67043328
        ),
        name="layers",
    )(x, values, rows, cols, count, w_first, w_second)


def shards(features, tile_values, tile_rows, tile_cols, tile_count, w_first, w_second):
    return both_layers(
        features.reshape(BLOCK_TILES, TILE, F), tile_values, tile_rows[0], tile_cols[0], tile_count, w_first, w_second
    )


def solution(mesh):
    return jax.shard_map(
        shards,
        mesh=mesh,
        in_specs=(
            P(("row", "col"), None),
            P("row", "col", None, None, None),
            P("row", "col", None),
            P("row", "col", None),
            P("row", "col"),
            P(),
            P(),
        ),
        out_specs=P(("row", "col"), None),
        check_vma=False,
    )
```

time: 794 us -> 143 us (0.18)
  waiting for transfers between devices: 355 us -> 0 us
  local copies, waits for them, and re-layouts: 181 us -> 1.87 us
  Pallas kernels: 0 us -> 140 us
  matrix products: 136 us -> 0 us
  other arithmetic: 102 us -> 0 us
  between operations: 16.9 us -> 0.66 us
    reduce_scatter x2 -> x0, waiting for transfers between devices: 296 us -> none  [propagate(): lax.psum_scatter(rounded, 'col', scatter_dimension=0, tiled=True)]
    pallas_call x0 -> x1, Pallas kernels: none -> 140 us  [both_layers(): pl.pallas_call(kernel, out_shape=jax.ShapeDtypeStruct((NODES, F), BF16),...]
    dot_general x20 -> x0, matrix products: 136 us -> none  [the longest x6 62.7 us: group_step(): placed = placed + jnp.dot(selector, low, preferred_element_type=jnp.float32)]
    while x12 -> x0, local copies, waits for them, and re-layouts: 93.7 us -> none
    add x6 -> x0, other arithmetic: 72.4 us -> none  [group_step(): return current + placed.reshape(out_tiles, tile_size, feature_width)]
    gather x31 -> x0, local copies, waits for them, and re-layouts: 71.9 us -> none  [the longest x6 29.6 us: group_step(): panel_tiles[source]]
    all_gather x2 -> x0, waiting for transfers between devices: 58.1 us -> none  [propagate(): lax.all_gather(inputs_now, 'row', axis=0, tiled=True)]
    convert_element_type x2 -> x0, other arithmetic: 18.1 us -> none  [propagate(): rounded = partial_value.reshape(-1, feature_width).astype(jnp.bfloat16)]
  transfers between devices with their start and end apart: 4 -> 0, of which waited for: 4 -> 0; matrix products, arithmetic and copies ran while one was open for 1% -> 0% of each run, Pallas kernels for 0% -> 0%
where the time goes in v2:
time: 143 us
  Pallas kernels  140 us (98%)
  local copies, waits for them, and re-layouts  1.87 us (1%)
    pallas_call x1, Pallas kernels, both_layers(): pl.pallas_call(kernel, out_shape=jax.ShapeDtypeStruct((NODES, F), BF16),...  140 us

profile of v2, /device:TPU:0, one launch (start us, length us, event | category | flops | bytes accessed | tf_op | source)
XLA Modules:
  0.0 142.9 jit_solution(6672239816975471418)
XLA Ops:
  0.7 140.3 %layers.1 = bf16[1024,256]{1,0:T(8,128)(2,1)} custom-call(bf16[8,128,256]{2,1,0:T(8,128)(2,1)} %bitcast.3, bf16[1,1,256,128,128]{4,3,2,1,0:T(8,128)(2,1)} %values_hbm.1, s32[1,256]{1,0:T(1,128)} %bitcast.4, s32[1,256]{1,0:T(1,128)} %bitcast.5, s32[1,1]{1,0:T(1,128)S(6)} %copy.9.tile_count, bf16[256,256]{1,0:T(8,128)(2,1)} %w_first.1, bf16[256,256]{1,0:T(8,128)(2,1)} %w_second.1), custom_call_target="tpu_custom_call" | custom-call | tf_op jit(solution)/shard_map/layers/pallas_call | solution.py:476
  141.0 1.9 %copy.10 = bf16[1024,256]{1,0:T(8,128)(2,1)} copy(bf16[1024,256]{1,0:T(8,128)(2,1)} %layers.1) | data formatting | bytes 1048576

commit v3 on v2

--- a/solution.py
+++ b/solution.py
@@ -21,10 +21,7 @@
     ((0, 1, 0, 512), (0, 1, 512, 512), (1, 1, 0, 256), (1, 1, 256, 256), (1, 1, 512, 256), (1, 1, 768, 256)),
     ((0, 1, 0, 1024), (1, 1, 0, 512), (1, 1, 512, 512)),
 )
-SPREADS = (
-    ((0, 1, 0, 8), (0, 1, 0, 8)),
-    ((0, 2, 0, 2), (0, 2, 2, 2), (0, 2, 4, 2), (0, 2, 6, 2)),
-)
+SPREADS = (((0, 8),), ((0, 2), (2, 2), (4, 2), (6, 2)))
 
 
 def remote(src, dst, send, recv, row, col):
@@ -39,9 +36,9 @@
 
 class Spread:
     def __init__(self, unit, panel, sems, row, col):
-        self.f0, self.nf, self.t0, self.tiles = unit
+        self.t0, self.tiles = unit
         self.panel, self.row, self.col = panel, row, col
-        self.send, self.recv, self.mate_send, self.mate_recv = sems
+        self.recv, self.send, self.mate_recv = sems
         self.z, self.core = row // 2, row % 2
         self.mate = self.z * 2 + 1 - self.core
         self.steps = ((self.z + 1) % SIDE * 2 + self.core, (self.z + 3) % SIDE * 2 + self.core)
@@ -52,10 +49,10 @@
 
     def part(self, block, which):
         half = self.tiles // 2
-        return self.panel.at[pl.ds(self.f0, self.nf), pl.ds(block * BLOCK_TILES + self.t0 + which * half, half)]
+        return self.panel.at[pl.ds(block * BLOCK_TILES + self.t0 + which * half, half)]
 
     def sized(self, tiles):
-        return self.panel.at[pl.ds(self.f0, self.nf), pl.ds(0, tiles)]
+        return self.panel.at[pl.ds(0, tiles)]
 
     def hop(self, way, order, block, which):
         piece = self.part(block, which)
@@ -63,7 +60,7 @@
 
     def share(self, block, which):
         piece = self.part(block, which)
-        remote(piece, piece, self.mate_send, self.mate_recv, self.mate, self.col).start()
+        remote(piece, piece, self.send, self.mate_recv, self.mate, self.col).start()
 
     def own(self):
         for order in range(2):
@@ -81,20 +78,13 @@
                 self.hop(way, 2, block, which)
             self.share(block, which)
 
-    def finish(self):
-        await_bytes(self.sized(4 * self.tiles), self.mate_recv)
-
-    def drain(self):
-        await_bytes(self.sized(3 * self.tiles), self.send)
-        await_bytes(self.sized(4 * self.tiles), self.mate_send)
-
 
 class Sum:
     def __init__(self, unit, part, got1, got2, sems, row, col):
         self.f0, self.nf, self.r0, self.rows = unit
         self.quarter = self.rows // 4
         self.part, self.got1, self.got2 = part, got1, got2
-        self.send1, self.recv1, self.send2, self.recv2 = sems
+        self.recv1, self.recv2, self.send = sems
         self.row = row
         self.y, self.x = col // SIDE, col % SIDE
 
@@ -132,7 +122,7 @@
         else:
             src = self.group(half, self.step(first, way), way)
         remote(
-            src, self.got1.at[half, way, kind], self.send1, self.recv1.at[half, min(kind, 1)],
+            src, self.got1.at[half, way, kind], self.send, self.recv1.at[half, min(kind, 1)],
             self.row, self.place(half, self.step(first, way), second),
         ).start()
 
@@ -145,7 +135,7 @@
         else:
             src = self.single(half, self.step(second, way), way)
         remote(
-            src, self.got2.at[half, way, kind], self.send2, self.recv2.at[half, min(kind, 1)],
+            src, self.got2.at[half, way, kind], self.send, self.recv2.at[half, min(kind, 1)],
             self.row, self.place(half, first, self.step(second, way)),
         ).start()
 
@@ -225,12 +215,8 @@
                     total = total + self.got2[half, 1 - h, RAW, f].astype(jnp.float32)
                     summed[self.f0 + f, self.lines(half, h)] = total.astype(BF16)
 
-    def drain(self):
-        await_bytes(self.got1, self.send1)
-        await_bytes(self.got2, self.send2)
-
-
-def kernel(x, values_hbm, tile_rows, tile_cols, tile_count, w_first, w_second, out, *scratch):
+
+def kernel(x, values_hbm, rows_hbm, cols_hbm, tile_count, w_first_hbm, w_second_hbm, out, *scratch):
     scratch = list(scratch)
 
     def take(number):
@@ -238,27 +224,26 @@
         del scratch[:number]
         return taken
 
-    values, runs, part, summed, staged, plan, plan_smem, values_sem, x_sem, plan_sem, out_sem = take(11)
-    inputs, hidden = take(2), take(1)[0]
+    values, runs, part, summed, staged, plan, plan_smem, tile_rows, tile_cols, w_first, w_second = take(11)
+    values_sem, x_sem, plan_sem, out_sem, small_sem, spread_send, share_recv, sum_send = take(8)
+    panels = [take(2), take(2)]
     row, col = lax.axis_index("row"), lax.axis_index("col")
     spreads = [
-        [Spread(unit, panel, take(4), row, col) for unit, panel in zip(SPREADS[0], inputs)],
-        [Spread(unit, hidden, take(4), row, col) for unit in SPREADS[1]],
+        [
+            [
+                Spread(unit, panels[layer][f], take(1) + [spread_send, share_recv.at[layer, f]], row, col)
+                for unit in SPREADS[layer]
+            ]
+            for f in range(2)
+        ]
+        for layer in range(2)
     ]
-    sums = [[Sum(unit, part, *take(2), take(4), row, col) for unit in UNITS[layer]] for layer in range(2)]
-
-    loads = [
-        pltpu.make_async_copy(
-            x.at[:, :, pl.ds(f * WIDE, WIDE)], inputs[f].at[0, pl.ds(row * BLOCK_TILES, BLOCK_TILES)], x_sem.at[f]
-        )
-        for f in range(2)
+    sums = [
+        [Sum(unit, part, *take(2), take(2) + [sum_send.at[layer]], row, col) for unit in UNITS[layer]]
+        for layer in range(2)
     ]
-    for load in loads:
-        load.start()
-    values_load = pltpu.make_async_copy(values_hbm.at[0, 0], values, values_sem)
-    values_load.start()
-
-    first_spread = spreads[0][0]
+
+    first_spread = spreads[0][0][0]
     first_sum = sums[0][0]
     partners = [(step, col) for step in first_spread.steps] + [(first_spread.mate, col)]
     for half, way in Sum.both:
@@ -267,39 +252,63 @@
     barrier = pltpu.get_barrier_semaphore()
     for to_row, to_col in partners:
         pl.semaphore_signal(barrier, inc=1, device_id=(to_row, to_col), device_id_type=MESH)
+
+    loads = [
+        pltpu.make_async_copy(
+            x.at[:, :, pl.ds(f * WIDE, WIDE)], panels[0][f].at[pl.ds(row * BLOCK_TILES, BLOCK_TILES)], x_sem.at[f]
+        )
+        for f in range(2)
+    ]
+    small = [
+        pltpu.make_async_copy(source, target, small_sem.at[i])
+        for i, (source, target) in enumerate(
+            ((rows_hbm, tile_rows), (cols_hbm, tile_cols), (w_first_hbm, w_first), (w_second_hbm, w_second))
+        )
+    ]
+    for copy in [loads[0]] + small[:2] + [loads[1]] + small[2:]:
+        copy.start()
+    values_load = pltpu.make_async_copy(values_hbm.at[0, 0], values, values_sem)
+    values_load.start()
     pl.semaphore_wait(barrier, len(partners))
     loads[0].wait()
-    spreads[0][0].own()
+    spreads[0][0][0].own()
+    for copy in small:
+        copy.wait()
 
     lane = lax.broadcasted_iota(jnp.int32, (1, SLOTS), 1)
-    key = jnp.where(lane < tile_count[0, 0], tile_rows[0] * 64 + tile_cols[0], lane + 8192)
+    key = jnp.where(lane < tile_count[0, 0], tile_rows[...] * 64 + tile_cols[...], lane + 8192)
     across = jnp.broadcast_to(key.astype(jnp.float32), (SLOTS, SLOTS))
     down = jnp.transpose(across)
     rank = jnp.sum(jnp.where(across < down, 1.0, 0.0), axis=1, keepdims=True)
-    lanes = lax.broadcasted_iota(jnp.int32, (SLOTS, SLOTS), 1)
+    lanes = lax.broadcasted_iota(jnp.int32, (SLOTS, SLOTS), 1).astype(jnp.float32)
     slots = lax.broadcasted_iota(jnp.int32, (SLOTS, SLOTS), 0).astype(jnp.float32)
-    chosen = rank == lanes.astype(jnp.float32)
-    order = jnp.sum(jnp.where(chosen, slots, 0.0), axis=0, keepdims=True)
-    ordered = jnp.sum(jnp.where(chosen, down, 0.0), axis=0, keepdims=True)
-    ends = jnp.sum(jnp.where(down < ((lanes + 1) * 64).astype(jnp.float32), 1.0, 0.0), axis=0, keepdims=True)
-    rest = jnp.zeros((5, SLOTS), jnp.float32)
-    plan[...] = jnp.concatenate([order, ordered, ends, rest], axis=0).astype(jnp.int32)
+
+    def pick(condition, what):
+        return jnp.sum(jnp.where(condition, what, 0.0), axis=0, keepdims=True).astype(jnp.int32)
+
+    order = pick(rank == lanes, slots)
+    ordered = pick(rank == lanes, down)
+    before = pick(rank == lanes - 1.0, down)
+    ends = pick(down < (lanes + 1.0) * 64.0, 1.0)
+    starts = pick(down < lanes * 64.0, 1.0)
+    same = jnp.where(jnp.right_shift(ordered, 6) == jnp.right_shift(before, 6), 1, 0)
+    run_of = jnp.where(ends == starts, SLOTS, ends - 1)
+    rest = jnp.zeros((4, SLOTS), jnp.int32)
+    plan[...] = jnp.concatenate([order, jnp.bitwise_and(ordered, 63), run_of, same, rest], axis=0)
     for f in range(2):
         runs[f, SLOTS] = jnp.zeros((TILE, WIDE), BF16)
     plan_copy = pltpu.make_async_copy(plan, plan_smem, plan_sem)
     plan_copy.start()
 
-    def multiply(panel, f, f0, first, last, total):
+    def multiply(panel, f, first, last, total):
         def block(it, total):
             for u in range(UNROLL):
                 at = it * UNROLL + u
                 slot = jnp.clip(plan_smem[0, at], 0, SLOTS - 1)
-                key = jnp.clip(plan_smem[1, at], 0, 64 * SLOTS - 1)
-                before = plan_smem[1, jnp.maximum(at - 1, 0)]
-                keep = jnp.where(key // 64 == before // 64, 1.0, 0.0)
-                right = panel[f, key % 64]
-                total = total * keep + jnp.dot(values[slot], right, preferred_element_type=jnp.float32)
-                runs[f0, at] = total.astype(BF16)
+                column = jnp.clip(plan_smem[1, at], 0, 63)
+                keep = jnp.where(plan_smem[3, at] == 1, 1.0, 0.0)
+                total = total * keep + jnp.dot(values[slot], panel[column], preferred_element_type=jnp.float32)
+                runs[f, at] = total.astype(BF16)
             return total
 
         return lax.fori_loop(first // UNROLL, last // UNROLL, block, total)
@@ -310,19 +319,16 @@
         tiles = unit.rows // 2 // TILE
         base = unit.r0 // TILE + half * tiles
 
-        @pl.loop(0, SIDE * tiles)
-        def _(i):
-            second, t = i // tiles, base + i % tiles
+        @pl.loop(0, SIDE, unroll=SIDE if tiles == 1 else 1)
+        def _(second):
             up, across = (second, first) if half == 0 else (first, second)
-            line = (up * SIDE + across) * BLOCK_TILES + t
-            end = plan_smem[2, line]
-            start = jnp.where(line == 0, 0, plan_smem[2, jnp.maximum(line - 1, 0)])
-            run = jnp.clip(jnp.where(end == start, SLOTS, end - 1), 0, SLOTS)
-            for f in range(unit.nf):
-                part[unit.f0 + f, up, across, pl.ds(pl.multiple_of(t * TILE, TILE), TILE)] = runs[unit.f0 + f, run]
+            for t in range(base, base + tiles):
+                run = jnp.clip(plan_smem[2, (up * SIDE + across) * BLOCK_TILES + t], 0, SLOTS)
+                for f in range(unit.f0, unit.f0 + unit.nf):
+                    part[f, up, across, pl.ds(t * TILE, TILE)] = runs[f, run]
 
     def weigh(unit, w, store):
-        @pl.loop(0, unit.rows // TILE)
+        @pl.loop(0, unit.rows // TILE, unroll=unit.rows // TILE)
         def _(i):
             t = unit.r0 // TILE + i
             lines = pl.ds(pl.multiple_of(t * TILE, TILE), TILE)
@@ -332,96 +338,115 @@
 
     def keep_hidden(t, block):
         for f in range(2):
-            hidden[f, row * BLOCK_TILES + t] = block[:, f * WIDE : (f + 1) * WIDE]
+            panels[1][f][row * BLOCK_TILES + t] = block[:, f * WIDE : (f + 1) * WIDE]
+
+    def write(t):
+        lines = pl.ds(pl.multiple_of(t * TILE, TILE), TILE)
+        return pltpu.make_async_copy(staged.at[lines], out.at[lines], out_sem)
 
     def keep_output(t, block):
         staged[pl.ds(pl.multiple_of(t * TILE, TILE), TILE)] = block
-
-    def write(unit):
-        lines = pl.ds(unit.r0, unit.rows)
-        return pltpu.make_async_copy(staged.at[lines], out.at[lines], out_sem.at[unit.r0 // 512])
-
-    a, b = spreads[0]
+        write(t).start()
+
+    def shared(layer, f):
+        await_bytes(panels[layer][f].at[pl.ds(0, 32)], share_recv.at[layer, f])
+
+    (a,), (b,) = spreads[0]
     a0, a1, b0, b1, b2, b3 = sums[0]
-    g0, g1, g2, g3 = spreads[1]
+    (g0, g1, g2, g3), (h0, h1, h2, h3) = spreads[1]
+    d, e0, e1 = sums[1]
     a.onward(0)
     loads[1].wait()
     b.own()
     a.onward(1)
     a.onward(2)
+    shared(0, 0)
     plan_copy.wait()
     values_load.wait()
-    a.finish()
-    total = multiply(inputs[0], 0, 0, 0, 128, empty)
+    total = multiply(panels[0][0], 0, 0, 128, empty)
+    total = multiply(panels[0][0], 0, 128, 256, total)
+    a0.open(fill)
     b.onward(0)
-    total = multiply(inputs[0], 0, 0, 128, 256, total)
+    b.onward(1)
+    a0.merge1()
+    b.onward(2)
+    shared(0, 1)
     a1.open(fill)
-    b.onward(1)
-    a0.open(fill)
-    b.onward(2)
-    b.finish()
-    total = multiply(inputs[1], 0, 1, 0, 256, empty)
-    a0.merge1()
-    b0.open(fill)
+    total = multiply(panels[0][1], 1, 0, 128, empty)
+    total = multiply(panels[0][1], 1, 128, 256, total)
     b1.open(fill)
     a0.turn()
+    b0.open(fill)
     b1.merge1()
     b0.merge1()
+    b2.open(fill)
+    b0.turn()
     a0.merge2()
     a1.merge1()
-    b0.turn()
+    b0.merge2()
     b1.turn()
-    b2.open(fill)
-    b0.merge2()
     a0.close(summed)
+    b3.open(fill)
+    b0.close(summed)
     b1.merge2()
-    b3.open(fill)
+    weigh(b0, w_first, keep_hidden)
+    h0.own()
     b2.merge1()
+    b3.merge1()
+    a1.turn()
+    g0.own()
     b1.close(summed)
     weigh(b1, w_first, keep_hidden)
-    b0.close(summed)
     g1.own()
-    weigh(b0, w_first, keep_hidden)
-    g0.own()
-    b3.merge1()
-    a1.turn()
     b2.turn()
+    h1.own()
     b3.turn()
     a1.merge2()
+    g0.onward(0)
     b2.merge2()
+    b3.merge2()
+    h1.onward(0)
+    h1.onward(1)
     g1.onward(0)
-    g0.onward(0)
-    b3.merge2()
     a1.close(summed)
     b2.close(summed)
     weigh(b2, w_first, keep_hidden)
-    g2.own()
     g0.onward(1)
     g1.onward(1)
+    g2.own()
     b3.close(summed)
     weigh(b3, w_first, keep_hidden)
     g3.own()
+    h2.own()
+    g2.onward(0)
+    g3.onward(0)
+    h3.own()
+    h0.onward(0)
+    g1.onward(2)
+    g2.onward(1)
     g0.onward(2)
-    g1.onward(2)
-    g0.finish()
-    g1.finish()
-    g2.onward(0)
-    g2.onward(1)
-    g3.onward(0)
     g3.onward(1)
     g2.onward(2)
-    g2.finish()
+    h1.onward(2)
+    h0.onward(1)
+    h2.onward(0)
     g3.onward(2)
-    for unit in sums[0]:
-        unit.drain()
-    g3.finish()
-
-    d, e0, e1 = sums[1]
-    total = multiply(hidden, 0, 0, 0, 256, empty)
+    h3.onward(0)
+    h2.onward(1)
+    shared(1, 0)
+    await_bytes(values.at[pl.ds(0, 240)], sum_send.at[0])
+
+    total = multiply(panels[1][0], 0, 0, 128, empty)
+    h2.onward(2)
+    h0.onward(2)
+    h3.onward(1)
+    total = multiply(panels[1][0], 0, 128, 256, total)
+    h3.onward(2)
     d.open(fill)
-    total = multiply(hidden, 1, 1, 0, 128, empty)
+    shared(1, 1)
+    total = multiply(panels[1][1], 1, 0, 128, empty)
     d.merge1()
-    total = multiply(hidden, 1, 1, 128, 256, total)
+    total = multiply(panels[1][1], 1, 128, 256, total)
     e1.open(fill)
     e0.open(fill)
     e1.merge1()
@@ -435,19 +460,15 @@
     d.close(summed)
     e1.close(summed)
     weigh(e1, w_second, keep_output)
-    write(e1).start()
     e0.close(summed)
     weigh(e0, w_second, keep_output)
-    write(e0).start()
-    for unit in spreads[0] + spreads[1] + sums[1]:
-        unit.drain()
-    write(e0).wait()
-    write(e1).wait()
+    await_bytes(values.at[pl.ds(0, 224)], spread_send)
+    await_bytes(values.at[pl.ds(0, 240)], sum_send.at[1])
+    await_bytes(staged, out_sem)
 
 
 def both_layers(x, values, rows, cols, count, w_first, w_second):
-    vmem, smem = pl.BlockSpec(memory_space=pltpu.VMEM), pl.BlockSpec(memory_space=pltpu.SMEM)
-    hbm = pl.BlockSpec(memory_space=pl.ANY)
+    smem, hbm = pl.BlockSpec(memory_space=pltpu.SMEM), pl.BlockSpec(memory_space=pl.ANY)
     dma = pltpu.SemaphoreType.DMA
     scratch = [
         pltpu.VMEM((SLOTS, TILE, TILE), BF16),
@@ -457,26 +478,34 @@
         pltpu.VMEM((NODES, F), BF16),
         pltpu.VMEM((8, SLOTS), jnp.int32),
         pltpu.SMEM((8, SLOTS), jnp.int32),
+        pltpu.VMEM((1, SLOTS), jnp.int32),
+        pltpu.VMEM((1, SLOTS), jnp.int32),
+        pltpu.VMEM((F, F), BF16),
+        pltpu.VMEM((F, F), BF16),
         dma,
         dma((2,)),
         dma,
+        dma,
+        dma((4,)),
+        dma,
+        dma((2, 2)),
         dma((2,)),
     ]
-    scratch += [pltpu.VMEM((halves, 64, TILE, WIDE), BF16) for halves in (1, 1, 2)]
+    scratch += [pltpu.VMEM((64, TILE, WIDE), BF16)] * 4
     for layer in range(2):
-        for _ in SPREADS[layer]:
-            scratch += [dma, dma((3,)), dma, dma]
+        for _ in SPREADS[layer] * 2:
+            scratch += [dma((3,))]
     for layer in range(2):
         for _, nf, _, rows_of in UNITS[layer]:
             scratch += [
                 pltpu.VMEM((2, 2, 3, nf, SIDE, rows_of // 4, WIDE), BF16),
                 pltpu.VMEM((2, 2, 3, nf, rows_of // 4, WIDE), BF16),
-                dma, dma((2, 2)), dma, dma((2, 2)),
+                dma((2, 2)), dma((2, 2)),
             ]
     return pl.pallas_call(
         kernel,
         out_shape=jax.ShapeDtypeStruct((NODES, F), BF16),
-        in_specs=[hbm, hbm, vmem, vmem, smem, vmem, vmem],
+        in_specs=[hbm, hbm, hbm, hbm, smem, hbm, hbm],
         out_specs=hbm,
         scratch_shapes=scratch,
         compiler_params=pltpu.CompilerParams(

time: 143 us -> 134 us (0.937)
  Pallas kernels: 140 us -> 131 us
    pallas_call x1, Pallas kernels: 140 us -> 131 us  [both_layers(): pl.pallas_call(kernel, out_shape=jax.ShapeDtypeStruct((NODES, F), BF16),...]
where the time goes in v3:
time: 134 us
  Pallas kernels  131 us (98%)
  local copies, waits for them, and re-layouts  1.87 us (1%)
    pallas_call x1, Pallas kernels, both_layers(): pl.pallas_call(kernel, out_shape=jax.ShapeDtypeStruct((NODES, F), BF16),...  131 us

profile of v3, /device:TPU:0, one launch (start us, length us, event | category | flops | bytes accessed | tf_op | source)
XLA Modules:
  0.0 133.9 jit_solution(7426070114654022633)
XLA Ops:
  0.7 131.4 %layers.1 = bf16[1024,256]{1,0:T(8,128)(2,1)} custom-call(bf16[8,128,256]{2,1,0:T(8,128)(2,1)} %bitcast.3, bf16[1,1,256,128,128]{4,3,2,1,0:T(8,128)(2,1)} %values_hbm.1, s32[1,256]{1,0:T(1,128)} %bitcast.4, s32[1,256]{1,0:T(1,128)} %bitcast.5, s32[1,1]{1,0:T(1,128)S(6)} %copy.9.tile_count, bf16[256,256]{1,0:T(8,128)(2,1)} %w_first_hbm.1, ...), custom_call_target="tpu_custom_call" | custom-call | tf_op jit(solution)/shard_map/layers/pallas_call | solution.py:505
  132.1 1.9 %copy.10 = bf16[1024,256]{1,0:T(8,128)(2,1)} copy(bf16[1024,256]{1,0:T(8,128)(2,1)} %layers.1) | data formatting | bytes 1048576

commit v4 on v3

--- a/solution.py
+++ b/solution.py
@@ -13,7 +13,7 @@
 NODES = 1024
 SIDE = 4
 BLOCK_TILES = NODES // TILE
-UNROLL = 32
+UNROLL = 128
 FAR, RAW, MERGED = 0, 1, 2
 BF16 = jnp.bfloat16
 

time: 134 us -> 133 us (level)
    pallas_call x1, Pallas kernels: 131 us -> 130 us  [both_layers(): pl.pallas_call(kernel, out_shape=jax.ShapeDtypeStruct((NODES, F), BF16),...]
where the time goes in v4:
time: 133 us
  Pallas kernels  130 us (98%)
  local copies, waits for them, and re-layouts  1.87 us (1%)
    pallas_call x1, Pallas kernels, both_layers(): pl.pallas_call(kernel, out_shape=jax.ShapeDtypeStruct((NODES, F), BF16),...  130 us

profile of v4, /device:TPU:0, one launch (start us, length us, event | category | flops | bytes accessed | tf_op | source)
XLA Modules:
  0.0 132.5 jit_solution(11056309138369603127)
XLA Ops:
  0.7 130.0 %layers.1 = bf16[1024,256]{1,0:T(8,128)(2,1)} custom-call(bf16[8,128,256]{2,1,0:T(8,128)(2,1)} %bitcast.3, bf16[1,1,256,128,128]{4,3,2,1,0:T(8,128)(2,1)} %values_hbm.1, s32[1,256]{1,0:T(1,128)} %bitcast.4, s32[1,256]{1,0:T(1,128)} %bitcast.5, s32[1,1]{1,0:T(1,128)S(6)} %copy.9.tile_count, bf16[256,256]{1,0:T(8,128)(2,1)} %w_first_hbm.1, ...), custom_call_target="tpu_custom_call" | custom-call | tf_op jit(solution)/shard_map/layers/pallas_call | solution.py:505
  130.7 1.9 %copy.10 = bf16[1024,256]{1,0:T(8,128)(2,1)} copy(bf16[1024,256]{1,0:T(8,128)(2,1)} %layers.1) | data formatting | bytes 1048576

commit v5 on v4

--- a/solution.py
+++ b/solution.py
@@ -24,6 +24,9 @@
 SPREADS = (((0, 8),), ((0, 2), (2, 2), (4, 2), (6, 2)))
 
 
+LAST = (1, 0, SPREADS[1][-1])
+
+
 def remote(src, dst, send, recv, row, col):
     return pltpu.make_async_remote_copy(
         src_ref=src, dst_ref=dst, send_sem=send, recv_sem=recv, device_id=(row, col), device_id_type=MESH
@@ -35,13 +38,15 @@
 
 
 class Spread:
-    def __init__(self, unit, panel, sems, row, col):
+    def __init__(self, unit, panel, sems, row, col, pair=False):
         self.t0, self.tiles = unit
+        self.pair = pair
         self.panel, self.row, self.col = panel, row, col
         self.recv, self.send, self.mate_recv = sems
         self.z, self.core = row // 2, row % 2
         self.mate = self.z * 2 + 1 - self.core
         self.steps = ((self.z + 1) % SIDE * 2 + self.core, (self.z + 3) % SIDE * 2 + self.core)
+        self.across = tuple(step + 1 - 2 * self.core for step in self.steps)
         self.groups = (((3, 0), (1, 1)), ((3, 1), (1, 0)), ((2, 0), (2, 1)))
 
     def at(self, distance, core):
@@ -76,7 +81,11 @@
             block = self.at(distance, self.core)
             if order == 0:
                 self.hop(way, 2, block, which)
-            self.share(block, which)
+                if self.pair:
+                    piece = self.part(block, which)
+                    remote(piece, piece, self.send, self.mate_recv, self.across[way], self.col).start()
+            if order < 2 or not self.pair:
+                self.share(block, which)
 
 
 class Sum:
@@ -231,7 +240,7 @@
     spreads = [
         [
             [
-                Spread(unit, panels[layer][f], take(1) + [spread_send, share_recv.at[layer, f]], row, col)
+                Spread(unit, panels[layer][f], take(1) + [spread_send, share_recv.at[layer, f]], row, col, (layer, f, unit) == LAST)
                 for unit in SPREADS[layer]
             ]
             for f in range(2)
@@ -245,7 +254,7 @@
 
     first_spread = spreads[0][0][0]
     first_sum = sums[0][0]
-    partners = [(step, col) for step in first_spread.steps] + [(first_spread.mate, col)]
+    partners = [(step, col) for step in first_spread.steps + first_spread.across + (first_spread.mate,)]
     for half, way in Sum.both:
         first, second = first_sum.spot(half)
         partners.append((row, first_sum.place(half, first_sum.step(first, way), second)))
@@ -417,9 +426,9 @@
     b3.close(summed)
     weigh(b3, w_first, keep_hidden)
     g3.own()
-    h2.own()
     g2.onward(0)
     g3.onward(0)
+    h2.own()
     h3.own()
     h0.onward(0)
     g1.onward(2)

time: 133 us -> 133 us (level)
  no operation moved by 1% of the time
where the time goes in v5:
time: 133 us
  Pallas kernels  131 us (98%)
  local copies, waits for them, and re-layouts  1.87 us (1%)
    pallas_call x1, Pallas kernels, both_layers(): pl.pallas_call(kernel, out_shape=jax.ShapeDtypeStruct((NODES, F), BF16),...  131 us

profile of v5, /device:TPU:0, one launch (start us, length us, event | category | flops | bytes accessed | tf_op | source)
XLA Modules:
  0.0 133.3 jit_solution(895430168740330337)
XLA Ops:
  0.7 130.8 %layers.1 = bf16[1024,256]{1,0:T(8,128)(2,1)} custom-call(bf16[8,128,256]{2,1,0:T(8,128)(2,1)} %bitcast.3, bf16[1,1,256,128,128]{4,3,2,1,0:T(8,128)(2,1)} %values_hbm.1, s32[1,256]{1,0:T(1,128)} %bitcast.4, s32[1,256]{1,0:T(1,128)} %bitcast.5, s32[1,1]{1,0:T(1,128)S(6)} %copy.9.tile_count, bf16[256,256]{1,0:T(8,128)(2,1)} %w_first_hbm.1, ...), custom_call_target="tpu_custom_call" | custom-call | tf_op jit(solution)/shard_map/layers/pallas_call | solution.py:514
  131.4 1.9 %copy.10 = bf16[1024,256]{1,0:T(8,128)(2,1)} copy(bf16[1024,256]{1,0:T(8,128)(2,1)} %layers.1) | data formatting | bytes 1048576

commit v6 on v4

--- a/solution.py
+++ b/solution.py
@@ -13,7 +13,6 @@
 NODES = 1024
 SIDE = 4
 BLOCK_TILES = NODES // TILE
-UNROLL = 128
 FAR, RAW, MERGED = 0, 1, 2
 BF16 = jnp.bfloat16
 
@@ -301,17 +300,13 @@
     plan_copy.start()
 
     def multiply(panel, f, first, last, total):
-        def block(it, total):
-            for u in range(UNROLL):
-                at = it * UNROLL + u
-                slot = jnp.clip(plan_smem[0, at], 0, SLOTS - 1)
-                column = jnp.clip(plan_smem[1, at], 0, 63)
-                keep = jnp.where(plan_smem[3, at] == 1, 1.0, 0.0)
-                total = total * keep + jnp.dot(values[slot], panel[column], preferred_element_type=jnp.float32)
-                runs[f, at] = total.astype(BF16)
-            return total
-
-        return lax.fori_loop(first // UNROLL, last // UNROLL, block, total)
+        for at in range(first, last):
+            slot = jnp.clip(plan_smem[0, at], 0, SLOTS - 1)
+            column = jnp.clip(plan_smem[1, at], 0, 63)
+            keep = jnp.where(plan_smem[3, at] == 1, 1.0, 0.0)
+            total = total * keep + jnp.dot(values[slot], panel[column], preferred_element_type=jnp.float32)
+            runs[f, at] = total.astype(BF16)
+        return total
 
     empty = jnp.zeros((TILE, WIDE), jnp.float32)
 
@@ -363,8 +358,7 @@
     shared(0, 0)
     plan_copy.wait()
     values_load.wait()
-    total = multiply(panels[0][0], 0, 0, 128, empty)
-    total = multiply(panels[0][0], 0, 128, 256, total)
+    multiply(panels[0][0], 0, 0, 256, empty)
     a0.open(fill)
     b.onward(0)
     b.onward(1)
@@ -372,8 +366,7 @@
     b.onward(2)
     shared(0, 1)
     a1.open(fill)
-    total = multiply(panels[0][1], 1, 0, 128, empty)
-    total = multiply(panels[0][1], 1, 128, 256, total)
+    multiply(panels[0][1], 1, 0, 256, empty)
     b1.open(fill)
     a0.turn()
     b0.open(fill)
@@ -436,11 +429,10 @@
     shared(1, 0)
     await_bytes(values.at[pl.ds(0, 240)], sum_send.at[0])
 
-    total = multiply(panels[1][0], 0, 0, 128, empty)
+    multiply(panels[1][0], 0, 0, 256, empty)
     h2.onward(2)
     h0.onward(2)
     h3.onward(1)
-    total = multiply(panels[1][0], 0, 128, 256, total)
     h3.onward(2)
     d.open(fill)
     shared(1, 1)

time: 133 us -> 133 us (level)
  no operation moved by 1% of the time
where the time goes in v6:
time: 133 us; the launch traced here: 132 us
  Pallas kernels  130 us (98%)
  local copies, waits for them, and re-layouts  1.87 us (1%)
    pallas_call x1, Pallas kernels, both_layers(): pl.pallas_call(kernel, out_shape=jax.ShapeDtypeStruct((NODES, F), BF16),...  130 us

profile of v6, /device:TPU:0, one launch (start us, length us, event | category | flops | bytes accessed | tf_op | source)
XLA Modules:
  0.0 132.5 jit_solution(2148296982838947773)
XLA Ops:
  0.7 130.0 %layers.1 = bf16[1024,256]{1,0:T(8,128)(2,1)} custom-call(bf16[8,128,256]{2,1,0:T(8,128)(2,1)} %bitcast.3, bf16[1,1,256,128,128]{4,3,2,1,0:T(8,128)(2,1)} %values_hbm.1, s32[1,256]{1,0:T(1,128)} %bitcast.4, s32[1,256]{1,0:T(1,128)} %bitcast.5, s32[1,1]{1,0:T(1,128)S(6)} %copy.9.tile_count, bf16[256,256]{1,0:T(8,128)(2,1)} %w_first_hbm.1, ...), custom_call_target="tpu_custom_call" | custom-call | tf_op jit(solution)/shard_map/layers/pallas_call | solution.py:497
  130.6 1.9 %copy.10 = bf16[1024,256]{1,0:T(8,128)(2,1)} copy(bf16[1024,256]{1,0:T(8,128)(2,1)} %layers.1) | data formatting | bytes 1048576
